TPU v7x, 16 devices: a 4x2x1 block of a 4x4x8 slice. The times are simulated.
16 devices in a mesh: dp: 2 (over y, z), tp: 8 (over x, core).
Axes of the slice: x: 4, y: 2, z: 1, core: 2. Of those that a mesh axis runs over, the one named last changes fastest.
The devices are a block of a 4x4x8 slice.
Arguments:
- k_local: bfloat16 [6, 1024, 16, 256], P('dp', 'tp'), parts along dimension 0
- v_local: bfloat16 [6, 1024, 16, 256], P('dp', 'tp'), parts along dimension 0
- k_global: bfloat16 [6, 1024, 16, 256], P('dp', 'tp'), parts along dimension 0
- v_global: bfloat16 [6, 1024, 16, 256], P('dp', 'tp'), parts along dimension 0
- x_token: bfloat16 [6, 3072], P('dp'), parts along dimension 0
- w_q: bfloat16 [2, 3072, 4096], P(None, None, 'tp')
- w_k: bfloat16 [2, 3072, 4096], P(None, None, 'tp')
- w_v: bfloat16 [2, 3072, 4096], P(None, None, 'tp')
- w_o: bfloat16 [2, 4096, 3072], P(None, 'tp')
- w_gate: bfloat16 [2, 3072, 24576], P(None, None, 'tp')
- w_up: bfloat16 [2, 3072, 24576], P(None, None, 'tp')
- w_down: bfloat16 [2, 24576, 3072], P(None, 'tp')
- norm_gain: float32 [2, 4, 3072], replicated
- qk_gain: float32 [2, 2, 256], replicated
Outputs:
- output 1: bfloat16 [6, 3072], P('dp'), parts along dimension 0
- output 2: bfloat16 [6, 1024, 16, 256], P('dp', None, 'tp'), parts along dimension 0
- output 3: bfloat16 [6, 1024, 16, 256], P('dp', None, 'tp'), parts along dimension 0
- output 4: bfloat16 [6, 1152, 16, 256], P('dp', None, 'tp'), parts along dimension 0
- output 5: bfloat16 [6, 1152, 16, 256], P('dp', None, 'tp'), parts along dimension 0
There are 2 independent parts. A program takes and returns all parts, laid end to end along the dimension named above; an argument that names none is the same for every part.
All inputs are finite; a program needn't handle non-finite values.
Results may differ from a plain program's by a relative error of at most 0.0149703.
Values are sent between devices in bfloat16 or wider.
A program may use at most 768 MiB of HBM per device.

v0:
```python
import jax
import jax.numpy as jnp
from jax import lax
from jax.sharding import PartitionSpec as P

WINDOW = 1024
NEW_SLOTS = 128
NORM_EPS = 1e-6
LOCAL_BASE = 10000.0
GLOBAL_BASE = 1000000.0
POS_SCALE = 8.0


def rms_norm(values, gain_vec):
    mean_sq = jnp.mean(values * values, axis=-1, keepdims=True)
    return values * lax.rsqrt(mean_sq + NORM_EPS) * (1.0 + gain_vec)


def rope_rotate(values, position, rope_base):
    head_dim = values.shape[-1]
    half_dim = head_dim // 2
    inv_freq = rope_base ** (-2.0 * jnp.arange(half_dim, dtype=jnp.float32) / head_dim)
    angles = position * inv_freq
    cos_part = jnp.cos(angles)
    sin_part = jnp.sin(angles)
    first_half = values[..., :half_dim]
    second_half = values[..., half_dim:]
    return jnp.concatenate([first_half * cos_part - second_half * sin_part, second_half * cos_part + first_half * sin_part], axis=-1)


def project_qkv(hidden, layer_idx, w_q, w_k, w_v, norm_gain, qk_gain, position, rope_base):
    batch_rows = hidden.shape[0]
    head_dim = qk_gain.shape[-1]
    normed = rms_norm(hidden, norm_gain[layer_idx, 0]).astype(jnp.bfloat16)
    q_proj = jnp.dot(normed, w_q[layer_idx], preferred_element_type=jnp.float32).reshape(batch_rows, -1, head_dim)
    k_proj = jnp.dot(normed, w_k[layer_idx], preferred_element_type=jnp.float32).reshape(batch_rows, -1, head_dim)
    v_proj = jnp.dot(normed, w_v[layer_idx], preferred_element_type=jnp.float32).reshape(batch_rows, -1, head_dim)
    q_new = rope_rotate(rms_norm(q_proj, qk_gain[layer_idx, 0]), position, rope_base).astype(jnp.bfloat16)
    k_new = rope_rotate(rms_norm(k_proj, qk_gain[layer_idx, 1]), position, rope_base).astype(jnp.bfloat16)
    return q_new, k_new, v_proj.astype(jnp.bfloat16)


def attend(q_new, key_blocks, value_blocks):
    batch_rows = q_new.shape[0]
    kv_heads = key_blocks[0].shape[2]
    head_dim = key_blocks[0].shape[3]
    q_grouped = q_new.reshape(batch_rows, kv_heads, -1, head_dim)
    scores = jnp.concatenate([jnp.einsum("bkgd,btkd->bkgt", q_grouped, key_block, preferred_element_type=jnp.float32) for key_block in key_blocks], axis=-1) * head_dim ** -0.5
    attn_prob = jax.nn.softmax(scores, axis=-1).astype(jnp.bfloat16)
    partial_outs = []
    offset = 0
    for value_block in value_blocks:
        span_len = value_block.shape[1]
        partial_outs.append(jnp.einsum("bkgt,btkd->bkgd", attn_prob[..., offset:offset + span_len], value_block, preferred_element_type=jnp.float32))
        offset += span_len
    return sum(partial_outs).astype(jnp.bfloat16).reshape(batch_rows, -1)


def finish_layer(hidden, layer_idx, attn_out, w_o, w_gate, w_up, w_down, norm_gain):
    attn_proj = lax.psum(jnp.dot(attn_out, w_o[layer_idx], preferred_element_type=jnp.float32), "tp")
    hidden = hidden + rms_norm(attn_proj, norm_gain[layer_idx, 1])
    normed = rms_norm(hidden, norm_gain[layer_idx, 2]).astype(jnp.bfloat16)
    gate_proj = jnp.dot(normed, w_gate[layer_idx], preferred_element_type=jnp.float32)
    up_proj = jnp.dot(normed, w_up[layer_idx], preferred_element_type=jnp.float32)
    gated_act = (jax.nn.gelu(gate_proj, approximate=True) * up_proj).astype(jnp.bfloat16)
    down_proj = lax.psum(jnp.dot(gated_act, w_down[layer_idx], preferred_element_type=jnp.float32), "tp")
    return hidden + rms_norm(down_proj, norm_gain[layer_idx, 3])


def move_window(cache_shard, groups):
    batch_rows, seq_dev, kv_heads, head_dim = cache_shard.shape
    kv_local = kv_heads // groups
    tail_len = min(WINDOW, seq_dev)
    src_count = -(-WINDOW // seq_dev)
    first_src = groups - src_count
    tail_piece = cache_shard[:, seq_dev - tail_len:]
    my_index = lax.axis_index("tp")
    src_block = my_index - first_src
    window_buf = jnp.zeros((batch_rows, src_count * tail_len, kv_local, head_dim), cache_shard.dtype)
    for round_idx in range(groups):
        dest_dev = (src_block + round_idx) % groups
        outgoing = lax.dynamic_slice_in_dim(tail_piece, dest_dev * kv_local, kv_local, axis=2)
        send_pairs = [(first_src + block_num, (block_num + round_idx) % groups) for block_num in range(src_count)]
        incoming = lax.ppermute(outgoing, "tp", send_pairs)
        recv_block = (my_index - round_idx) % groups
        placed = lax.dynamic_update_slice_in_dim(window_buf, incoming, jnp.minimum(recv_block, src_count - 1) * tail_len, axis=1)
        window_buf = jnp.where(recv_block < src_count, placed, window_buf)
    return window_buf[:, src_count * tail_len - WINDOW:]


def solution(mesh):
    groups = mesh.shape["tp"]
    cache_in = P("dp", "tp", None, None)
    cache_out = P("dp", None, "tp", None)
    token_spec = P("dp", None)
    col_split = P(None, None, "tp")
    row_split = P(None, "tp", None)
    replicated = P()

    def per_device(k_local, v_local, k_global, v_global, x_token, w_q, w_k, w_v, w_o, w_gate, w_up, w_down, norm_gain, qk_gain):
        seq_len = k_global.shape[1] * groups
        slot_shift = seq_len % WINDOW
        k_window = move_window(k_local, groups)
        v_window = move_window(v_local, groups)
        moved_k = lax.all_to_all(k_global, "tp", 2, 1, tiled=True)
        moved_v = lax.all_to_all(v_global, "tp", 2, 1, tiled=True)
        hidden = x_token.astype(jnp.float32)
        q_new, k_new, v_new = project_qkv(hidden, 0, w_q, w_k, w_v, norm_gain, qk_gain, float(seq_len), LOCAL_BASE)
        k_circular = lax.dynamic_update_slice_in_dim(jnp.roll(k_window, slot_shift, axis=1), k_new[:, None], slot_shift, axis=1)
        v_circular = lax.dynamic_update_slice_in_dim(jnp.roll(v_window, slot_shift, axis=1), v_new[:, None], slot_shift, axis=1)
        attn_out = attend(q_new, [k_circular], [v_circular])
        hidden = finish_layer(hidden, 0, attn_out, w_o, w_gate, w_up, w_down, norm_gain)
        hidden = hidden.astype(jnp.bfloat16).astype(jnp.float32)
        q_new, k_new, v_new = project_qkv(hidden, 1, w_q, w_k, w_v, norm_gain, qk_gain, seq_len / POS_SCALE, GLOBAL_BASE)
        attn_out = attend(q_new, [moved_k, k_new[:, None]], [moved_v, v_new[:, None]])
        hidden = finish_layer(hidden, 1, attn_out, w_o, w_gate, w_up, w_down, norm_gain)
        zero_slots = jnp.zeros((moved_k.shape[0], NEW_SLOTS - 1) + moved_k.shape[2:], moved_k.dtype)
        k_cache = jnp.concatenate([moved_k, k_new[:, None], zero_slots], axis=1)
        v_cache = jnp.concatenate([moved_v, v_new[:, None], zero_slots], axis=1)
        return hidden.astype(jnp.bfloat16), k_circular, v_circular, k_cache, v_cache

    return jax.shard_map(per_device, mesh=mesh, in_specs=(cache_in, cache_in, cache_in, cache_in, token_spec, col_split, col_split, col_split, row_split, col_split, col_split, row_split, replicated, replicated), out_specs=(token_spec, cache_out, cache_out, cache_out, cache_out), check_vma=False)
```

profile of v0, /device:TPU:113, one launch (start us, length us, event | category | flops | bytes accessed | tf_op | source)
XLA Modules:
  0.0 390.7 jit_solution(2691980286704477438)
XLA Ops:
  0.8 8.5 %constant_dynamic-slice_fusion.5 = (bf16[3,128,2,256]{3,2,1,0:T(2,128)(2,1)}, bf16[3,128,2,256]{3,2,1,0:T(2,128)(2,1)}, bf16[3,128,2,256]{3,2,1,0:T(2,128)(2,1)}...) fusion(bf16[3,128,16,256]{3,2,1,0:T(8,128)(2,1)} %param.14, ...), kind=kLoop, calls=%fused_computation.150 | loop fusion | bytes 6291488 | tf_op jit(solution)/shard_map/dynamic_slice | solution.py:82
  9.2 3.8 collective-permute-start
  21.8 5.4 %all-to-all-start = ((bf16[3,128,16,256]{3,1,0,2:T(8,128)(2,1)}), bf16[3,128,16,256]{3,1,0,2:T(8,128)(2,1)S(1)}, u32[]{:S(2)}, u32[]{:S(2)}) async-start(bf16[3,128,16,256]{3,1,0,2:T(8,128)(2,1)} %copy.89), calls=%async_computation | async-start | bytes 6291456 | tf_op jit(solution)/shard_map/all_to_all | solution.py:105
  27.6 6.0 %slice_bitcast_fusion.4 = (bf16[512,3072]{0,1:T(8,128)(2,1)}, bf16[512,3072]{0,1:T(8,128)(2,1)}) fusion(bf16[2,3072,512]{2,1,0:T(8,128)(2,1)} %param.20), kind=kLoop, calls=%fused_computation.44 | loop fusion | bytes 12582912 | tf_op jit(solution)/shard_map/dot_general | solution.py:36
  33.6 4.6 %copy.84 = bf16[512,3072]{1,0:T(8,128)(2,1)} copy(bf16[512,3072]{0,1:T(8,128)(2,1)} %get-tuple-element.15) | data formatting | bytes 6291456 | tf_op jit(solution)/shard_map/dot_general | solution.py:36
  41.1 6.0 %slice_bitcast_fusion.2 = (bf16[512,3072]{0,1:T(8,128)(2,1)}, bf16[512,3072]{0,1:T(8,128)(2,1)}) fusion(bf16[2,3072,512]{2,1,0:T(8,128)(2,1)} %param.19), kind=kLoop, calls=%fused_computation.41 | loop fusion | bytes 12582912 | tf_op jit(solution)/shard_map/dot_general | solution.py:35
  47.1 4.6 %copy.83 = bf16[512,3072]{1,0:T(8,128)(2,1)} copy(bf16[512,3072]{0,1:T(8,128)(2,1)} %get-tuple-element.14) | data formatting | bytes 6291456 | tf_op jit(solution)/shard_map/dot_general | solution.py:35
  54.8 5.1 %constant_dynamic-slice_fusion.10 = (bf16[3,128,2,256]{3,2,1,0:T(2,128)(2,1)}, bf16[3,128,2,256]{3,2,1,0:T(2,128)(2,1)}, bf16[3,128,2,256]{3,2,1,0:T(2,128)(2,1)...) fusion(bf16[3,128,16,256]{3,2,1,0:T(8,128)(2,1)S(1)} %copy-done, ...), kind=kLoop, calls=%fused_computation.156 | loop fusion | bytes 6291488 | tf_op jit(solution)/shard_map/dynamic_slice | solution.py:82
  59.9 5.9 %slice_bitcast_fusion = (bf16[512,3072]{0,1:T(8,128)(2,1)}, bf16[512,3072]{0,1:T(8,128)(2,1)}) fusion(bf16[2,3072,512]{2,1,0:T(8,128)(2,1)} %param.21), kind=kLoop, calls=%fused_computation.39 | loop fusion | bytes 12582912 | tf_op jit(solution)/shard_map/dot_general | solution.py:37
  65.8 4.6 %copy.86 = bf16[512,3072]{1,0:T(8,128)(2,1)} copy(bf16[512,3072]{0,1:T(8,128)(2,1)} %get-tuple-element.12) | data formatting | bytes 6291456 | tf_op jit(solution)/shard_map/dot_general | solution.py:37
  73.6 4.7 %copy.91 = bf16[512,3072]{1,0:T(8,128)(2,1)} copy(bf16[512,3072]{0,1:T(8,128)(2,1)} %get-tuple-element.16) | data formatting | bytes 6291456 | tf_op jit(solution)/shard_map/dot_general | solution.py:36
  78.3 4.6 %copy.88 = bf16[512,3072]{1,0:T(8,128)(2,1)} copy(bf16[512,3072]{0,1:T(8,128)(2,1)} %get-tuple-element.13) | data formatting | bytes 6291456 | tf_op jit(solution)/shard_map/dot_general | solution.py:35
  83.0 4.6 %copy.99 = bf16[3,128,16,256]{3,1,0,2:T(8,128)(2,1)} copy(bf16[3,128,16,256]{3,2,1,0:T(8,128)(2,1)} %param.17) | data formatting | bytes 6291456 | tf_op args[3]
  87.6 5.2 %copy.102 = bf16[512,3072]{1,0:T(8,128)(2,1)} copy(bf16[512,3072]{0,1:T(8,128)(2,1)} %get-tuple-element.11) | data formatting | bytes 6291456 | tf_op jit(solution)/shard_map/dot_general | solution.py:37
  109.1 5.7 %collective-permute-done.6 = bf16[3,128,2,256]{3,2,1,0:T(2,128)(2,1)S(1)} collective-permute-done((bf16[3,128,2,256]{3,2,1,0:T(2,128)(2,1)S(1)}, bf16[3,128,2,256]{3,2,1,0:T(2,128)(2,1)S(1)}, u32[]{:S(2)}, u32[]{:S(2)}) %collective-permute-start.6) | collective-permute-done | bytes 393248 | tf_op jit(solution)/shard_map/ppermute | solution.py:84
  121.6 3.3 broadcast.366.clone
  125.9 10.7 %collective-permute-start.14 = (bf16[3,128,2,256]{3,2,1,0:T(2,128)(2,1)}, bf16[3,128,2,256]{3,2,1,0:T(2,128)(2,1)}, u32[]{:S(2)}, u32[]{:S(2)}) collective-permute-start(bf16[3,128,2,256]{3,2,1,0:T(2,128)(2,1)} %get-tuple-element.32), channel_id=1, source_target_pairs={{0,6},{1,7},{2,0},{3,1},{4,2},{5,3},{6,4},{7,5},{8,14},{9,15},{10,... | collective-permute-start | bytes 1179656 | tf_op jit(solution)/shard_map/ppermute | solution.py:84
  138.8 3.3 collective-permute-start.15
  150.9 4.1 %collective-permute-done.14 = bf16[3,128,2,256]{3,2,1,0:T(2,128)(2,1)} collective-permute-done((bf16[3,128,2,256]{3,2,1,0:T(2,128)(2,1)}, bf16[3,128,2,256]{3,2,1,0:T(2,128)(2,1)}, u32[]{:S(2)}, u32[]{:S(2)}) %collective-permute-start.14) | collective-permute-done | bytes 393248 | tf_op jit(solution)/shard_map/ppermute | solution.py:84
  165.2 20.9 %psum.28 = f32[3,3072]{1,0:T(4,128)S(1)} all-reduce(f32[3,3072]{1,0:T(4,128)S(1)} %fusion.34), channel_id=1, replica_groups=mesh['dp'=2,'tp'=8] {'tp'}, use_global_device_ids=true, to_apply=%region_5.6 | all-reduce | flops 9216 | bytes 73728 | tf_op jit(solution)/shard_map/psum | solution.py:60
  186.4 7.8 %fusion.81 = f32[3,3072]{1,0:T(4,128)S(1)} fusion(bf16[2,3072,3072]{2,1,0:T(8,128)(2,1)} %param.23, f32[3,3072]{1,0:T(4,128)S(1)} %get-tuple-element.10, f32[3072]{0:T(1024)S(1)} %bitcast.188, f32[3]{0:T(128)S(1)} %add_rsqrt_fusion.9), kind=kOutput, calls=%fused_computation.103 | convolution fusion | flops 56724480 | bytes 18960396 | tf_op jit(solution)/shard_map/dot_general | solution.py:63
  194.2 14.3 %fusion.8 = f32[3,3072]{1,0:T(4,128)S(1)} fusion(bf16[2,3072,3072]{2,1,0:T(8,128)(2,1)} %param.25, f32[3,3072]{1,0:T(4,128)S(1)} %fusion.81, bf16[2,3072,3072]{2,1,0:T(8,128)(2,1)} %param.24, f32[3,3072]{1,0:T(4,128)S(1)} %get-tuple-element.10, f32[3072]{0:T(1024)S(1)} %bitcast.189, f32[3]{0:T(128)S(1)} %add_rsqrt_fusion.9), kind=kOutput, calls=%fused_computation.8 | convolution fusion | flops 113292288 | bytes 37871628 | tf_op jit(solution)/shard_map/dot_general | solution.py:66
  208.5 24.4 %psum.29 = f32[3,3072]{1,0:T(4,128)S(1)} all-reduce(f32[3,3072]{1,0:T(4,128)S(1)} %fusion.8), channel_id=1, replica_groups=mesh['dp'=2,'tp'=8] {'tp'}, use_global_device_ids=true, to_apply=%region_8.9 | all-reduce | flops 9216 | bytes 73728 | tf_op jit(solution)/shard_map/psum | solution.py:66
  234.9 7.9 %all-to-all-start.1 = ((bf16[3,128,16,256]{3,1,0,2:T(8,128)(2,1)}), bf16[3,128,16,256]{3,1,0,2:T(8,128)(2,1)}, u32[]{:S(2)}, u32[]{:S(2)}) async-start(bf16[3,128,16,256]{3,1,0,2:T(8,128)(2,1)} %copy.99), calls=%async_computation.1 | async-start | bytes 6291456 | tf_op jit(solution)/shard_map/all_to_all | solution.py:106
  247.3 5.2 %copy.90 = bf16[3,8,128,2,256]{4,3,2,1,0:T(2,128)(2,1)S(1)} copy(bf16[3,8,128,2,256]{4,2,0,3,1:T(8,128)(2,1)} %bitcast.168) | data formatting | bytes 6291456 | tf_op jit(solution)/shard_map/all_to_all | solution.py:105
  253.9 26.3 %all-to-all-done.1 = bf16[3,128,16,256]{3,1,0,2:T(8,128)(2,1)} async-done(((bf16[3,128,16,256]{3,1,0,2:T(8,128)(2,1)}), bf16[3,128,16,256]{3,1,0,2:T(8,128)(2,1)}, u32[]{:S(2)}, u32[]{:S(2)}) %all-to-all-start.1) | async-done | bytes 3145760 | tf_op jit(solution)/shard_map/all_to_all | solution.py:106
  280.1 6.9 %copy.100 = bf16[3,8,128,2,256]{4,3,2,1,0:T(2,128)(2,1)} copy(bf16[3,8,128,2,256]{4,2,0,3,1:T(8,128)(2,1)} %bitcast.47) | data formatting | bytes 6291456 | tf_op jit(solution)/shard_map/all_to_all | solution.py:106
  293.3 22.2 %psum.30 = f32[3,3072]{1,0:T(4,128)S(1)} all-reduce(f32[3,3072]{1,0:T(4,128)S(1)} %fusion.32), channel_id=1, replica_groups=mesh['dp'=2,'tp'=8] {'tp'}, use_global_device_ids=true, to_apply=%region_15.16 | all-reduce | flops 9216 | bytes 73728 | tf_op jit(solution)/shard_map/psum | solution.py:60
  315.8 7.8 %fusion.93 = f32[3,3072]{1,0:T(4,128)S(1)} fusion(bf16[2,3072,3072]{2,1,0:T(8,128)(2,1)} %param.23, f32[3,3072]{1,0:T(4,128)S(1)} %get-tuple-element.6, f32[3072]{0:T(1024)S(1)} %bitcast.186, f32[3]{0:T(128)S(1)} %add_rsqrt_fusion.5), kind=kOutput, calls=%fused_computation.113 | convolution fusion | flops 56724480 | bytes 18960396 | tf_op jit(solution)/shard_map/dot_general | solution.py:63
  323.6 14.4 %fusion.2 = f32[3,3072]{1,0:T(4,128)S(1)} fusion(bf16[2,3072,3072]{2,1,0:T(8,128)(2,1)} %param.25, f32[3,3072]{1,0:T(4,128)S(1)} %fusion.93, bf16[2,3072,3072]{2,1,0:T(8,128)(2,1)} %param.24, f32[3,3072]{1,0:T(4,128)S(1)} %get-tuple-element.6, f32[3072]{0:T(1024)S(1)} %bitcast.187, f32[3]{0:T(128)S(1)} %add_rsqrt_fusion.5), kind=kOutput, calls=%fused_computation.2 | convolution fusion | flops 113292288 | bytes 37871628 | tf_op jit(solution)/shard_map/dot_general | solution.py:66
  338.0 24.1 %psum.31 = f32[3,3072]{1,0:T(4,128)S(1)} all-reduce(f32[3,3072]{1,0:T(4,128)S(1)} %fusion.2), channel_id=1, replica_groups=mesh['dp'=2,'tp'=8] {'tp'}, use_global_device_ids=true, to_apply=%region_18.19 | all-reduce | flops 9216 | bytes 73728 | tf_op jit(solution)/shard_map/psum | solution.py:66
  363.0 27.4 %maximum_maximum_fusion.1 = (bf16[3,1152,2,256]{3,2,1,0:T(2,128)(2,1)}, bf16[3,1152,2,256]{3,2,1,0:T(2,128)(2,1)}) fusion(bf16[3,1,2,256]{3,2,1,0:T(2,128)(2,1)S(1)} %copy.104, bf16[3,1024,2,256]{3,2,1,0:T(2,128)(2,1)} %bitcast.176, bf16[1152]{0:T(1024)(128)(2,1)S(1)} %pad.5.clone, bf16[3,1,2,256]{3,2,1,0:T(2,128)(2,1)S(1)} %copy.103, ...), kind=kLoop, calls=%fused_computation.21 | loop fusion | flops 7077888 | bytes 13377792 | tf_op jit(solution)/shard_map/concatenate | solution.py:119
  (145 shorter events, 78.5 us)
Async XLA Ops:
  0.7 18.3 %copy-start.4 = (bf16[3,128,16,256]{3,2,1,0:T(8,128)(2,1)S(1)}, bf16[3,128,16,256]{3,2,1,0:T(8,128)(2,1)}, u32[]{:S(2)}) copy-start(bf16[3,128,16,256]{3,2,1,0:T(8,128)(2,1)} %param.16) | copy-start | bytes 9437188
  9.2 83.7 %collective-permute-start = (bf16[3,128,2,256]{3,2,1,0:T(2,128)(2,1)}, bf16[3,128,2,256]{3,2,1,0:T(2,128)(2,1)}, u32[]{:S(2)}, u32[]{:S(2)}) collective-permute-start(bf16[3,128,2,256]{3,2,1,0:T(2,128)(2,1)} %get-tuple-element.23), channel_id=1, source_target_pairs={{0,0},{1,1},{2,2},{3,3},{4,4},{5,5},{6,6},{7,7},{8,8},{9,9},{10,10... | collective-permute-start | bytes 1179656 | tf_op jit(solution)/shard_map/ppermute | solution.py:84
  13.1 86.0 %collective-permute-start.1 = (bf16[3,128,2,256]{3,2,1,0:T(2,128)(2,1)}, bf16[3,128,2,256]{3,2,1,0:T(2,128)(2,1)}, u32[]{:S(2)}, u32[]{:S(2)}) collective-permute-start(bf16[3,128,2,256]{3,2,1,0:T(2,128)(2,1)} %get-tuple-element.22), channel_id=1, source_target_pairs={{0,1},{1,2},{2,3},{3,4},{4,5},{5,6},{6,7},{7,0},{8,9},{9,10},{10,1... | collective-permute-start | bytes 1179656 | tf_op jit(solution)/shard_map/ppermute | solution.py:84
  15.8 85.4 %collective-permute-start.2 = (bf16[3,128,2,256]{3,2,1,0:T(2,128)(2,1)}, bf16[3,128,2,256]{3,2,1,0:T(2,128)(2,1)}, u32[]{:S(2)}, u32[]{:S(2)}) collective-permute-start(bf16[3,128,2,256]{3,2,1,0:T(2,128)(2,1)} %get-tuple-element.21), channel_id=1, source_target_pairs={{0,2},{1,3},{2,4},{3,5},{4,6},{5,7},{6,0},{7,1},{8,10},{9,11},{10,... | collective-permute-start | bytes 1179656 | tf_op jit(solution)/shard_map/ppermute | solution.py:84
  17.2 86.6 %collective-permute-start.3 = (bf16[3,128,2,256]{3,2,1,0:T(2,128)(2,1)}, bf16[3,128,2,256]{3,2,1,0:T(2,128)(2,1)}, u32[]{:S(2)}, u32[]{:S(2)}) collective-permute-start(bf16[3,128,2,256]{3,2,1,0:T(2,128)(2,1)} %get-tuple-element.20), channel_id=1, source_target_pairs={{0,3},{1,4},{2,5},{3,6},{4,7},{5,0},{6,1},{7,2},{8,11},{9,12},{10,... | collective-permute-start | bytes 1179656 | tf_op jit(solution)/shard_map/ppermute | solution.py:84
  18.8 86.5 %collective-permute-start.4 = (bf16[3,128,2,256]{3,2,1,0:T(2,128)(2,1)}, bf16[3,128,2,256]{3,2,1,0:T(2,128)(2,1)}, u32[]{:S(2)}, u32[]{:S(2)}) collective-permute-start(bf16[3,128,2,256]{3,2,1,0:T(2,128)(2,1)} %get-tuple-element.19), channel_id=1, source_target_pairs={{0,4},{1,5},{2,6},{3,7},{4,0},{5,1},{6,2},{7,3},{8,12},{9,13},{10,... | collective-permute-start | bytes 1179656 | tf_op jit(solution)/shard_map/ppermute | solution.py:84
  21.8 5.5 %copy-start.15 = (f32[2,4,3072]{2,1,0:T(4,128)S(1)}, f32[2,4,3072]{2,1,0:T(4,128)}, u32[]{:S(2)}) copy-start(f32[2,4,3072]{2,1,0:T(4,128)} %param.26) | copy-start | bytes 294916
  21.8 5.6 %copy-start.6 = (bf16[3,3072]{1,0:T(4,128)(2,1)S(1)}, bf16[3,3072]{1,0:T(4,128)(2,1)}, u32[]{:S(2)}) copy-start(bf16[3,3072]{1,0:T(4,128)(2,1)} %param.18) | copy-start | bytes 55300
  21.8 211.5 %all-to-all-start = ((bf16[3,128,16,256]{3,1,0,2:T(8,128)(2,1)}), bf16[3,128,16,256]{3,1,0,2:T(8,128)(2,1)S(1)}, u32[]{:S(2)}, u32[]{:S(2)}) async-start(bf16[3,128,16,256]{3,1,0,2:T(8,128)(2,1)} %copy.89), calls=%async_computation | async-start | bytes 6291456 | tf_op jit(solution)/shard_map/all_to_all | solution.py:105
  51.7 3.1 copy-start.5
  92.9 6.2 %copy-start.10 = (bf16[3,128,2,256]{3,2,1,0:T(2,128)(2,1)S(1)}, bf16[3,128,2,256]{3,2,1,0:T(2,128)(2,1)}, u32[]{:S(2)}) copy-start(bf16[3,128,2,256]{3,2,1,0:T(2,128)(2,1)} %get-tuple-element.24) | copy-start | bytes 1179652
  92.9 8.4 %copy-start.8 = (bf16[3,128,2,256]{3,2,1,0:T(2,128)(2,1)S(1)}, bf16[3,128,2,256]{3,2,1,0:T(2,128)(2,1)}, u32[]{:S(2)}) copy-start(bf16[3,128,2,256]{3,2,1,0:T(2,128)(2,1)} %get-tuple-element.17) | copy-start | bytes 1179652
  93.0 10.8 %copy-start.14 = (bf16[3,128,2,256]{3,2,1,0:T(2,128)(2,1)S(1)}, bf16[3,128,2,256]{3,2,1,0:T(2,128)(2,1)}, u32[]{:S(2)}) copy-start(bf16[3,128,2,256]{3,2,1,0:T(2,128)(2,1)} %get-tuple-element.31) | copy-start | bytes 1179652
  93.0 12.3 %copy-start.13 = (bf16[3,128,2,256]{3,2,1,0:T(2,128)(2,1)S(1)}, bf16[3,128,2,256]{3,2,1,0:T(2,128)(2,1)}, u32[]{:S(2)}) copy-start(bf16[3,128,2,256]{3,2,1,0:T(2,128)(2,1)} %get-tuple-element.30) | copy-start | bytes 1179652
  93.0 14.6 %collective-permute-start.5 = (bf16[3,128,2,256]{3,2,1,0:T(2,128)(2,1)}, bf16[3,128,2,256]{3,2,1,0:T(2,128)(2,1)S(1)}, u32[]{:S(2)}, u32[]{:S(2)}) collective-permute-start(bf16[3,128,2,256]{3,2,1,0:T(2,128)(2,1)} %get-tuple-element.18), channel_id=1, source_target_pairs={{0,5},{1,6},{2,7},{3,0},{4,1},{5,2},{6,3},{7,4},{8,13},{9,14},{10,... | collective-permute-start | bytes 1179656 | tf_op jit(solution)/shard_map/ppermute | solution.py:84
  97.6 10.0 %copy-start.12 = (bf16[3,128,2,256]{3,2,1,0:T(2,128)(2,1)S(1)}, bf16[3,128,2,256]{3,2,1,0:T(2,128)(2,1)}, u32[]{:S(2)}) copy-start(bf16[3,128,2,256]{3,2,1,0:T(2,128)(2,1)} %get-tuple-element.29) | copy-start | bytes 1179652
  99.1 15.8 %copy-start.11 = (bf16[3,128,2,256]{3,2,1,0:T(2,128)(2,1)S(1)}, bf16[3,128,2,256]{3,2,1,0:T(2,128)(2,1)}, u32[]{:S(2)}) copy-start(bf16[3,128,2,256]{3,2,1,0:T(2,128)(2,1)} %get-tuple-element.28) | copy-start | bytes 1179652
  99.1 15.7 %collective-permute-start.6 = (bf16[3,128,2,256]{3,2,1,0:T(2,128)(2,1)S(1)}, bf16[3,128,2,256]{3,2,1,0:T(2,128)(2,1)S(1)}, u32[]{:S(2)}, u32[]{:S(2)}) collective-permute-start(bf16[3,128,2,256]{3,2,1,0:T(2,128)(2,1)S(1)} %copy-done.10), channel_id=1, source_target_pairs={{0,6},{1,7},{2,0},{3,1},{4,2},{5,3},{6,4},{7,5},{8,14},{9,15},{10,... | collective-permute-start | bytes 1179656 | tf_op jit(solution)/shard_map/ppermute | solution.py:84
  101.2 15.7 %copy-start.9 = (bf16[3,128,2,256]{3,2,1,0:T(2,128)(2,1)S(1)}, bf16[3,128,2,256]{3,2,1,0:T(2,128)(2,1)}, u32[]{:S(2)}) copy-start(bf16[3,128,2,256]{3,2,1,0:T(2,128)(2,1)} %get-tuple-element.27) | copy-start | bytes 1179652
  101.2 15.7 %collective-permute-start.7 = (bf16[3,128,2,256]{3,2,1,0:T(2,128)(2,1)S(1)}, bf16[3,128,2,256]{3,2,1,0:T(2,128)(2,1)S(1)}, u32[]{:S(2)}, u32[]{:S(2)}) collective-permute-start(bf16[3,128,2,256]{3,2,1,0:T(2,128)(2,1)S(1)} %copy-done.8), channel_id=1, source_target_pairs={{0,7},{1,0},{2,1},{3,2},{4,3},{5,4},{6,5},{7,6},{8,15},{9,8},{10,9... | collective-permute-start | bytes 1179656 | tf_op jit(solution)/shard_map/ppermute | solution.py:84
  103.8 17.7 %collective-permute-start.8 = (bf16[3,128,2,256]{3,2,1,0:T(2,128)(2,1)S(1)}, bf16[3,128,2,256]{3,2,1,0:T(2,128)(2,1)S(1)}, u32[]{:S(2)}, u32[]{:S(2)}) collective-permute-start(bf16[3,128,2,256]{3,2,1,0:T(2,128)(2,1)S(1)} %copy-done.14), channel_id=1, source_target_pairs={{0,0},{1,1},{2,2},{3,3},{4,4},{5,5},{6,6},{7,7},{8,8},{9,9},{10,10... | collective-permute-start | bytes 1179656 | tf_op jit(solution)/shard_map/ppermute | solution.py:84
  105.3 20.6 %collective-permute-start.9 = (bf16[3,128,2,256]{3,2,1,0:T(2,128)(2,1)S(1)}, bf16[3,128,2,256]{3,2,1,0:T(2,128)(2,1)S(1)}, u32[]{:S(2)}, u32[]{:S(2)}) collective-permute-start(bf16[3,128,2,256]{3,2,1,0:T(2,128)(2,1)S(1)} %copy-done.13), channel_id=1, source_target_pairs={{0,1},{1,2},{2,3},{3,4},{4,5},{5,6},{6,7},{7,0},{8,9},{9,10},{10,1... | collective-permute-start | bytes 1179656 | tf_op jit(solution)/shard_map/ppermute | solution.py:84
  107.6 13.8 %copy-start.7 = (bf16[3,128,2,256]{3,2,1,0:T(2,128)(2,1)S(1)}, bf16[3,128,2,256]{3,2,1,0:T(2,128)(2,1)}, u32[]{:S(2)}) copy-start(bf16[3,128,2,256]{3,2,1,0:T(2,128)(2,1)} %get-tuple-element.26) | copy-start | bytes 1179652
  107.7 31.2 %collective-permute-start.10 = (bf16[3,128,2,256]{3,2,1,0:T(2,128)(2,1)S(1)}, bf16[3,128,2,256]{3,2,1,0:T(2,128)(2,1)S(1)}, u32[]{:S(2)}, u32[]{:S(2)}) collective-permute-start(bf16[3,128,2,256]{3,2,1,0:T(2,128)(2,1)S(1)} %copy-done.12), channel_id=1, source_target_pairs={{0,2},{1,3},{2,4},{3,5},{4,6},{5,7},{6,0},{7,1},{8,10},{9,11},{10,... | collective-permute-start | bytes 1179656 | tf_op jit(solution)/shard_map/ppermute | solution.py:84
  114.8 29.4 %collective-permute-start.11 = (bf16[3,128,2,256]{3,2,1,0:T(2,128)(2,1)S(1)}, bf16[3,128,2,256]{3,2,1,0:T(2,128)(2,1)S(1)}, u32[]{:S(2)}, u32[]{:S(2)}) collective-permute-start(bf16[3,128,2,256]{3,2,1,0:T(2,128)(2,1)S(1)} %copy-done.11), channel_id=1, source_target_pairs={{0,3},{1,4},{2,5},{3,6},{4,7},{5,0},{6,1},{7,2},{8,11},{9,12},{10,... | collective-permute-start | bytes 1179656 | tf_op jit(solution)/shard_map/ppermute | solution.py:84
  116.9 29.5 %collective-permute-start.12 = (bf16[3,128,2,256]{3,2,1,0:T(2,128)(2,1)S(1)}, bf16[3,128,2,256]{3,2,1,0:T(2,128)(2,1)S(1)}, u32[]{:S(2)}, u32[]{:S(2)}) collective-permute-start(bf16[3,128,2,256]{3,2,1,0:T(2,128)(2,1)S(1)} %copy-done.9), channel_id=1, source_target_pairs={{0,4},{1,5},{2,6},{3,7},{4,0},{5,1},{6,2},{7,3},{8,12},{9,13},{10,... | collective-permute-start | bytes 1179656 | tf_op jit(solution)/shard_map/ppermute | solution.py:84
  120.6 4.3 %copy-start = (bf16[3,1024,2,256]{3,2,1,0:T(2,128)(2,1)}, bf16[3,1024,2,256]{3,2,1,0:T(2,128)(2,1)S(1)}, u32[]{:S(2)}) copy-start(bf16[3,1024,2,256]{3,2,1,0:T(2,128)(2,1)S(1)} %constant_dynamic-update-slice_fusion) | copy-start | bytes 9437188
  121.5 27.1 %collective-permute-start.13 = (bf16[3,128,2,256]{3,2,1,0:T(2,128)(2,1)S(1)}, bf16[3,128,2,256]{3,2,1,0:T(2,128)(2,1)S(1)}, u32[]{:S(2)}, u32[]{:S(2)}) collective-permute-start(bf16[3,128,2,256]{3,2,1,0:T(2,128)(2,1)S(1)} %copy-done.7), channel_id=1, source_target_pairs={{0,5},{1,6},{2,7},{3,0},{4,1},{5,2},{6,3},{7,4},{8,13},{9,14},{10,... | collective-permute-start | bytes 1179656 | tf_op jit(solution)/shard_map/ppermute | solution.py:84
  125.9 29.1 %collective-permute-start.14 = (bf16[3,128,2,256]{3,2,1,0:T(2,128)(2,1)}, bf16[3,128,2,256]{3,2,1,0:T(2,128)(2,1)}, u32[]{:S(2)}, u32[]{:S(2)}) collective-permute-start(bf16[3,128,2,256]{3,2,1,0:T(2,128)(2,1)} %get-tuple-element.32), channel_id=1, source_target_pairs={{0,6},{1,7},{2,0},{3,1},{4,2},{5,3},{6,4},{7,5},{8,14},{9,15},{10,... | collective-permute-start | bytes 1179656 | tf_op jit(solution)/shard_map/ppermute | solution.py:84
  138.8 18.7 %collective-permute-start.15 = (bf16[3,128,2,256]{3,2,1,0:T(2,128)(2,1)}, bf16[3,128,2,256]{3,2,1,0:T(2,128)(2,1)}, u32[]{:S(2)}, u32[]{:S(2)}) collective-permute-start(bf16[3,128,2,256]{3,2,1,0:T(2,128)(2,1)} %get-tuple-element.25), channel_id=1, source_target_pairs={{0,7},{1,0},{2,1},{3,2},{4,3},{5,4},{6,5},{7,6},{8,15},{9,8},{10,9... | collective-permute-start | bytes 1179656 | tf_op jit(solution)/shard_map/ppermute | solution.py:84
  234.9 45.2 %all-to-all-start.1 = ((bf16[3,128,16,256]{3,1,0,2:T(8,128)(2,1)}), bf16[3,128,16,256]{3,1,0,2:T(8,128)(2,1)}, u32[]{:S(2)}, u32[]{:S(2)}) async-start(bf16[3,128,16,256]{3,1,0,2:T(8,128)(2,1)} %copy.99), calls=%async_computation.1 | async-start | bytes 6291456 | tf_op jit(solution)/shard_map/all_to_all | solution.py:106
  242.8 3.1 copy-start.3
  (3 other events, 7.5 us)
where the time goes:
time: 398 us; the launch traced here: 391 us
  blocking collectives  91.5 us (23%)
  local copies, waits for them, and re-layouts  87.2 us (22%)
  matrix products  69.5 us (17%)
  other arithmetic  56.1 us (14%)
  starting transfers between devices  48.1 us (12%)
  waiting for transfers between devices  36.4 us (9%)
    psum x2, blocking collectives, finish_layer(): lax.psum(jnp.dot(gated_act, w_down[layer_idx], preferred_element_type=jnp...  48.5 us
    psum x2, blocking collectives, finish_layer(): lax.psum(jnp.dot(attn_out, w_o[layer_idx], preferred_element_type=jnp.flo...  43.1 us
    ppermute x16, starting transfers between devices, move_window(): incoming = lax.ppermute(outgoing, 'tp', send_pairs)  34.8 us
    dot_general x2, matrix products, finish_layer(): jnp.dot(gated_act, w_down[layer_idx], preferred_element_type=jnp.float32)  28.7 us
    concatenate x1, other arithmetic, per_device(): v_cache = jnp.concatenate([moved_v, v_new[:, None], zero_slots], axis=1)  27.4 us
    all_to_all x1, waiting for transfers between devices, per_device(): moved_v = lax.all_to_all(v_global, 'tp', 2, 1, tiled=True)  26.3 us
    select_n x16, other arithmetic, move_window(): window_buf = jnp.where(recv_block < src_count, placed, window_buf)  25.3 us
    dot_general x3, local copies, waits for them, and re-layouts, project_qkv(): jnp.dot(normed, w_v[layer_idx], preferred_element_type=jnp.float32)  15.8 us
  transfers between devices with their start and end apart: 18, of which 4 were waited for; matrix products, arithmetic and copies ran while one was open for 35% of the time, Pallas kernels for 0%

commit v1 on v0

v1 whole, which is shorter than its diff:
```python
import functools

import jax
import jax.numpy as jnp
import numpy as np
from jax import lax
from jax.experimental import pallas as pl
from jax.experimental.pallas import tpu as pltpu
from jax.sharding import PartitionSpec as P

WINDOW = 1024
NEW_SLOTS = 128
NORM_EPS = 1e-6
ROPE_BASES = (10000.0, 1000000.0)
POS_SCALES = (1.0, 8.0)
NEG = -3.0e38
MESH = pl.DeviceIdType.MESH
LANES = 128
ROWS = 8
RING = 8
CHUNK = 512
HALVES = 2
FIRST_UNITS = 2
ROUND_UNITS = (1, 1, 1, 1, 3, 1, 1)
ROUNDS = len(ROUND_UNITS)


def rms_norm(values, gain_vec):
    mean_sq = jnp.mean(values * values, axis=-1, keepdims=True)
    return values * lax.rsqrt(mean_sq + NORM_EPS) * (1.0 + gain_vec)


def kernel(cfg, *refs):
    groups, layers, batch, seq_dev, heads, head_dim, width, ff_dev = cfg
    n_in, n_out = 2 * len(range(4)) + 11, 5
    ins, outs, scr = refs[:n_in], refs[n_in:n_in + n_out], refs[n_in + n_out:]
    views, caches = ins[:4], ins[4:8]
    x_hbm, wq, wk, wv, wo, wg, wu, wd, ng_hbm, qk_hbm, rope_hbm = ins[8:]
    cache_out, h_out = outs[:4], outs[4]
    (ring, wo_buf, kv, x_vm, ng, qkg, rope, h_ref, lhs, acc, q_all, st_all, o_all, part, rs_all, ag_all,
     ring_sem, wo_sem, kv_sem, small_sem, self_sem, bulk_send, bulk_recv, r_send, r_recv) = scr
    me = lax.axis_index("tp")
    per_tile = heads // 2
    pairs = per_tile // 2
    seq = seq_dev * groups
    half_dim = head_dim // 2
    ff_items = ff_dev // CHUNK
    wd_items = width // CHUNK
    per_layer = 3 + 2 * ff_items + wd_items
    items = layers * per_layer

    def issue(item):
        item = jnp.asarray(item, jnp.int32)
        layer = item // per_layer
        r = item % per_layer
        slot = item % RING
        dst = ring.at[slot]
        sem = ring_sem.at[slot]
        for pos, ref in enumerate((wq, wk, wv)):
            @pl.when(r == pos)
            def _(ref=ref):
                pltpu.make_async_copy(ref.at[layer], dst, sem).start()
        for par, ref in enumerate((wg, wu)):
            @pl.when((r >= 3) & (r < 3 + 2 * ff_items) & ((r - 3) % 2 == par))
            def _(ref=ref):
                col = pl.multiple_of(jnp.clip((r - 3) // 2, 0, ff_items - 1) * CHUNK, CHUNK)
                pltpu.make_async_copy(ref.at[layer, :, pl.ds(col, CHUNK)], dst, sem).start()

        @pl.when(r >= 3 + 2 * ff_items)
        def _():
            col = pl.multiple_of(jnp.clip(r - 3 - 2 * ff_items, 0, wd_items - 1) * CHUNK, CHUNK)
            pltpu.make_async_copy(wd.at[layer, :, pl.ds(col, CHUNK)], dst, sem).start()

    def stream(first, count):
        def step(t, carry):
            item = first + t
            slot = item % RING
            pltpu.make_async_copy(wq.at[0], ring.at[slot], ring_sem.at[slot]).wait()
            acc[t] = jnp.dot(lhs[...], ring[slot], preferred_element_type=jnp.float32)

            @pl.when(item + RING < items)
            def _():
                issue(item + RING)
            return carry
        lax.fori_loop(0, count, step, 0)

    small = [pltpu.make_async_copy(s, d, small_sem.at[n]) for n, (s, d) in enumerate(
        ((x_hbm, x_vm), (ng_hbm, ng), (qk_hbm, qkg), (rope_hbm, rope)))]
    for c in small:
        c.start()
    for n in range(3):
        issue(n)
    kv_copies = [pltpu.make_async_copy(caches[n], kv.at[n], kv_sem.at[n]) for n in range(4)]
    wo_copies = [pltpu.make_async_copy(wo.at[n], wo_buf, wo_sem.at[n]) for n in range(layers)]
    kv_copies[0].start()
    kv_copies[1].start()
    wo_copies[0].start()
    for n in range(3, RING):
        issue(n)

    barrier = pltpu.get_barrier_semaphore()
    for k in range(1, groups):
        pl.semaphore_signal(barrier, inc=1, device_id={"tp": (me + k) % groups}, device_id_type=MESH)
    pl.semaphore_wait(barrier, groups - 1)

    span = seq_dev // HALVES
    units = [(c, b, f) for c in range(4) for b in range(batch) for f in range(HALVES)]
    chips = groups // 2
    order = [(dx, dc) for dc in range(2) for dx in (1, chips - 1, *range(2, chips - 1))] + [(0, 1)]
    chip, core = me // 2, me % 2

    def peer(dx, dc):
        return ((chip + dx) % chips) * 2 + (core + dc) % 2

    def view_of(c, owner, b, start, size):
        return views[c].at[b, pl.ds(start, size), owner // pairs, :, owner % pairs]

    queue = list(units)

    def bulk(count):
        for _ in range(min(count, len(queue))):
            c, b, f = queue.pop(0)
            for k, (dx, dc) in enumerate(order):
                dst = peer(dx, dc)
                pltpu.make_async_remote_copy(
                    view_of(c, dst, b, f * span, span),
                    cache_out[c].at[b, pl.ds(me * seq_dev + f * span, span)],
                    bulk_send.at[c, k], bulk_recv.at[c, k],
                    device_id={"tp": dst}, device_id_type=MESH).start()

    bulk(FIRST_UNITS)
    self_copies = [pltpu.make_async_copy(
        view_of(c, me, b, 0, seq_dev), cache_out[c].at[b, pl.ds(me * seq_dev, seq_dev)], self_sem.at[c, b])
        for c in range(4) for b in range(batch)]
    for c in self_copies:
        c.start()
    kv_copies[2].start()
    kv_copies[3].start()

    sent = []

    def send(rnd, src_of, dst_ref):
        got = []
        for k in range(1, groups):
            d = (me + k) % groups
            c = pltpu.make_async_remote_copy(src_of(d), dst_ref.at[me], r_send.at[rnd, k], r_recv.at[rnd, k],
                                             device_id={"tp": d}, device_id_type=MESH)
            c.start()
            got.append(c)
        sent.extend(got)
        return got

    row = lax.broadcasted_iota(jnp.int32, (ROWS, LANES), 0)
    lane = lax.broadcasted_iota(jnp.int32, (ROWS, LANES), 1)
    even = lax.broadcasted_iota(jnp.int32, (ROWS, 1), 0) % 2 == 0
    lane_head = lane % heads
    own = (lane_head == 2 * me + row % 2) & (row < 2 * batch)
    col_tiles = seq_dev * heads // LANES
    row64 = lax.broadcasted_iota(jnp.int32, (groups * ROWS, LANES), 0)
    lane64 = lax.broadcasted_iota(jnp.int32, (groups * ROWS, LANES), 1)
    head_hit = (lane64 % heads) == 2 * (row64 // ROWS) + row64 % 2
    hits = [jnp.tile(head_hit & ((row64 % ROWS) // 2 == b), (1, col_tiles)) for b in range(batch)]
    wide_row = lax.broadcasted_iota(jnp.int32, (ROWS, seq_dev * heads), 0)
    wide_col = lax.broadcasted_iota(jnp.int32, (ROWS, seq_dev * heads), 1)
    paired = (wide_col % 2 == wide_row % 2) & (wide_row < 2 * batch)

    def fold(x, op):
        out = x[:, :LANES]
        for n in range(1, x.shape[1] // LANES):
            out = op(out, x[:, n * LANES:(n + 1) * LANES])
        shift = heads
        while shift < LANES:
            out = op(out, pltpu.roll(out, shift, 1))
            shift *= 2
        return out

    def rope_rotate(x, layer):
        cos, sin = rope[layer, 0:1, :], rope[layer, 1:2, :]
        a, b = x[:, :half_dim], x[:, half_dim:]
        return jnp.concatenate([a * cos - b * sin, b * cos + a * sin], axis=-1)

    def pick(y):
        return jnp.where(even, y[:, :head_dim], y[:, head_dim:])

    def all_reduce(rnd, layer, slot):
        got = send(rnd, lambda d: part.at[slot, d], rs_all.at[slot])
        bulk(ROUND_UNITS[(rnd % ROUNDS)])
        rs_all[slot, me] = part[slot, me]
        for c in got:
            c.wait_recv()
        total = rs_all[slot, 0]
        for s in range(1, groups):
            total = total + rs_all[slot, s]
        ag_all[slot, me] = total
        got = send(rnd + 1, lambda d: ag_all.at[slot, me], ag_all.at[slot])
        bulk(ROUND_UNITS[(rnd + 1) % ROUNDS])
        for c in got:
            c.wait_recv()
        return jnp.concatenate([ag_all[slot, s] for s in range(groups)], axis=-1)

    for c in small:
        c.wait()
    x = x_vm[...].astype(jnp.float32)
    wide8 = lax.broadcasted_iota(jnp.int32, (ROWS, width), 0) // 2
    h0 = jnp.zeros((ROWS, width), jnp.float32)
    for b in range(batch):
        h0 = jnp.where(wide8 == b, jnp.broadcast_to(x[b:b + 1], (ROWS, width)), h0)
    h_ref[...] = h0

    new_rows = []
    for layer in range(layers):
        rnd = layer * ROUNDS
        base = layer * per_layer
        lhs[...] = rms_norm(h_ref[...], ng[layer, 0:1, :]).astype(jnp.bfloat16)
        stream(base, 3)
        q = rope_rotate(rms_norm(pick(acc[0]), qkg[layer, 0:1, :]), layer).astype(jnp.bfloat16).astype(jnp.float32)
        q_all[layer, me] = q
        got = send(rnd, lambda d: q_all.at[layer, me], q_all.at[layer])
        bulk(ROUND_UNITS[0])
        k_new = rope_rotate(rms_norm(pick(acc[1]), qkg[layer, 1:2, :]), layer).astype(jnp.bfloat16).astype(jnp.float32)
        v_new = pick(acc[2]).astype(jnp.bfloat16).astype(jnp.float32)
        new_rows.append((k_new, v_new))
        scale = head_dim ** -0.5
        s_new = jnp.sum(q * k_new, axis=-1, keepdims=True) * scale
        kv_copies[2 * layer].wait()
        kv_copies[2 * layer + 1].wait()
        for c in got:
            c.wait_recv()
        q64 = q_all[layer].reshape(groups * ROWS, head_dim).astype(jnp.bfloat16)
        scores = jnp.zeros((ROWS, seq_dev * heads), jnp.float32)
        for b in range(batch):
            s = lax.dot_general(q64, kv[2 * layer, b], (((1,), (1,)), ((), ())), preferred_element_type=jnp.float32)
            s = jnp.where(hits[b], s, 0.0)
            for d in range(groups):
                scores = scores + s[d * ROWS:(d + 1) * ROWS]
        valid = paired
        if layer == 0:
            valid = valid & (me * seq_dev + wide_col // heads >= seq + 1 - WINDOW)
        scores = jnp.where(valid, scores * scale, NEG)
        m_loc = fold(scores, jnp.maximum)
        m_loc = jnp.where(own, jnp.maximum(m_loc, s_new), m_loc)
        ex = jnp.where(valid, jnp.exp(scores - jnp.tile(m_loc, (1, col_tiles))), 0.0)
        l_loc = fold(ex, jnp.add)
        l_loc = jnp.where(own, l_loc + jnp.exp(s_new - m_loc), l_loc)
        st_all[layer, me] = jnp.where(lane < LANES // 2, m_loc, l_loc)
        got = send(rnd + 1, lambda d: st_all.at[layer, me], st_all.at[layer])
        bulk(ROUND_UNITS[1])
        for c in got:
            c.wait_recv()
        stats = [st_all[layer, s] for s in range(groups)]
        low = lane < LANES // 2
        ms = [jnp.where(low, t, pltpu.roll(t, LANES // 2, 1)) for t in stats]
        ls = [jnp.where(low, pltpu.roll(t, LANES // 2, 1), t) for t in stats]
        m_all = functools.reduce(jnp.maximum, ms)
        l_all = functools.reduce(jnp.add, [l * jnp.exp(m - m_all) for m, l in zip(ms, ls)])
        l_all = jnp.where(row < 2 * batch, jnp.maximum(l_all, 1e-30), 1.0)
        prob = jnp.where(valid, jnp.exp(scores - jnp.tile(m_all, (1, col_tiles))) / jnp.tile(l_all, (1, col_tiles)), 0.0)
        p_new = jnp.where(own & (lane < heads), jnp.exp(jnp.minimum(s_new - m_all, 0.0)) / l_all, 0.0)
        p_new = jnp.sum(p_new, axis=-1, keepdims=True).astype(jnp.bfloat16).astype(jnp.float32)
        prob64 = jnp.concatenate([prob] * groups, axis=0)
        o_part = jnp.zeros((groups * ROWS, head_dim), jnp.float32)
        for b in range(batch):
            o_part = o_part + jnp.dot(jnp.where(hits[b], prob64, 0.0).astype(jnp.bfloat16), kv[2 * layer + 1, b],
                                      preferred_element_type=jnp.float32)
        o_all[layer, 0] = o_part.reshape(groups, ROWS, head_dim)
        got = send(rnd + 2, lambda d: o_all.at[layer, 0, d], o_all.at[layer, 1])
        bulk(ROUND_UNITS[2])
        o_all[layer, 1, me] = o_all[layer, 0, me]
        for c in got:
            c.wait_recv()
        o = p_new * v_new
        for s in range(groups):
            o = o + o_all[layer, 1, s]
        o = o.astype(jnp.bfloat16).astype(jnp.float32)
        o = jnp.concatenate([jnp.where(even, o, 0.0), jnp.where(even, 0.0, o)], axis=-1).astype(jnp.bfloat16)
        wo_copies[layer].wait()
        piece = width // groups
        for d in range(groups):
            y = jnp.dot(o, wo_buf[:, d * piece:(d + 1) * piece], preferred_element_type=jnp.float32)
            part[2 * layer, d] = y + jnp.where(even, pltpu.roll(y, ROWS - 1, 0), pltpu.roll(y, 1, 0))
        if layer + 1 < layers:
            wo_copies[layer + 1].start()
        hidden = h_ref[...] + rms_norm(all_reduce(rnd + 3, layer, 2 * layer), ng[layer, 1:2, :])
        h_ref[...] = hidden
        lhs[...] = rms_norm(hidden, ng[layer, 2:3, :]).astype(jnp.bfloat16)
        stream(base + 3, 2 * ff_items)
        for n in range(ff_items):
            lhs[:, n * CHUNK:(n + 1) * CHUNK] = (
                jax.nn.gelu(acc[2 * n], approximate=True) * acc[2 * n + 1]).astype(jnp.bfloat16)
        stream(base + 3 + 2 * ff_items, wd_items)
        full = jnp.concatenate([acc[n] for n in range(wd_items)], axis=-1)
        for d in range(groups):
            part[2 * layer + 1, d] = full[:, d * piece:(d + 1) * piece]
        hidden = h_ref[...] + rms_norm(all_reduce(rnd + 5, layer, 2 * layer + 1), ng[layer, 3:4, :])
        h_ref[...] = hidden.astype(jnp.bfloat16).astype(jnp.float32)

    bulk(len(queue))
    for b in range(batch):
        h_out[b:b + 1, :] = h_ref[2 * b:2 * b + 1, :].astype(jnp.bfloat16)
    zeros = jnp.zeros((NEW_SLOTS - 1, 2, 2, LANES), jnp.bfloat16)
    for c in (2, 3):
        for b in range(batch):
            cache_out[c][b, seq + 1:] = zeros
    for c in sent:
        c.wait_send()
    for c in self_copies:
        c.wait()
    for c in range(4):
        for k, (dx, dc) in enumerate(order):
            src = peer(-dx % chips, dc)
            region = cache_out[c].at[0:batch, pl.ds(src * seq_dev, seq_dev)]
            whole = pltpu.make_async_remote_copy(region, region, bulk_send.at[c, k], bulk_recv.at[c, k],
                                                 device_id={"tp": peer(dx, dc)}, device_id_type=MESH)
            whole.wait_recv()
            whole.wait_send()
    slots = (seq % WINDOW, seq)
    for layer in range(layers):
        for n in range(2):
            for b in range(batch):
                for ct in range(2):
                    cache_out[2 * layer + n][b, slots[layer], ct] = new_rows[layer][n][
                        2 * b:2 * b + 2, ct * LANES:(ct + 1) * LANES].astype(jnp.bfloat16)


def solution(mesh):
    groups = mesh.shape["tp"]
    cache_in = P("dp", "tp", None, None)
    cache_out = P("dp", None, "tp", None)
    token_spec = P("dp", None)
    col_split = P(None, None, "tp")
    row_split = P(None, "tp", None)
    replicated = P()

    def per_device(k_local, v_local, k_global, v_global, x_token, w_q, w_k, w_v, w_o, w_gate, w_up, w_down, norm_gain, qk_gain):
        batch, seq_dev, heads, head_dim = k_local.shape
        layers, width, _ = w_q.shape
        ff_dev = w_gate.shape[2]
        seq = seq_dev * groups
        tiles, pairs, cols = heads // 8, 4, head_dim // LANES
        caches = (k_local, v_local, k_global, v_global)
        views = [c.reshape(batch, seq_dev, tiles, pairs, 2, cols, LANES).transpose(0, 1, 2, 5, 3, 4, 6) for c in caches]
        flat = [c.reshape(batch, seq_dev * heads, head_dim) for c in caches]
        inv_freq = [b ** (-2.0 * np.arange(head_dim // 2) / head_dim) for b in ROPE_BASES]
        angles = [seq / s * f for s, f in zip(POS_SCALES, inv_freq)]
        rope = jnp.asarray(np.stack([np.stack([np.cos(a), np.sin(a)]) for a in angles]), jnp.float32)
        any_spec = pl.BlockSpec(memory_space=pl.ANY)
        vmem_spec = pl.BlockSpec(memory_space=pltpu.VMEM)
        cfg = (groups, layers, batch, seq_dev, heads, head_dim, width, ff_dev)
        slots = (WINDOW, WINDOW, seq + NEW_SLOTS, seq + NEW_SLOTS)
        piece = width // groups
        rounds = layers * ROUNDS
        res = pl.pallas_call(
            functools.partial(kernel, cfg),
            in_specs=[any_spec] * 19,
            out_specs=[vmem_spec] * 5,
            out_shape=[pltpu.VMEM((batch, s, 2, 2, LANES), jnp.bfloat16) for s in slots]
            + [jax.ShapeDtypeStruct((batch, width), jnp.bfloat16)],
            scratch_shapes=[
                pltpu.VMEM((RING, width, CHUNK), jnp.bfloat16),
                pltpu.VMEM((w_o.shape[1], width), jnp.bfloat16),
                pltpu.VMEM((4, batch, seq_dev * heads, head_dim), jnp.bfloat16),
                pltpu.VMEM(x_token.shape, jnp.bfloat16),
                pltpu.VMEM(norm_gain.shape, jnp.float32),
                pltpu.VMEM(qk_gain.shape, jnp.float32),
                pltpu.VMEM(rope.shape, jnp.float32),
                pltpu.VMEM((ROWS, width), jnp.float32),
                pltpu.VMEM((ROWS, width), jnp.bfloat16),
                pltpu.VMEM((2 * ff_dev // CHUNK, ROWS, CHUNK), jnp.float32),
                pltpu.VMEM((layers, groups, ROWS, head_dim), jnp.float32),
                pltpu.VMEM((layers, groups, ROWS, LANES), jnp.float32),
                pltpu.VMEM((layers, 2, groups, ROWS, head_dim), jnp.float32),
                pltpu.VMEM((2 * layers, groups, ROWS, piece), jnp.float32),
                pltpu.VMEM((2 * layers, groups, ROWS, piece), jnp.float32),
                pltpu.VMEM((2 * layers, groups, ROWS, piece), jnp.float32),
                pltpu.SemaphoreType.DMA((RING,)),
                pltpu.SemaphoreType.DMA((layers,)),
                pltpu.SemaphoreType.DMA((4,)),
                pltpu.SemaphoreType.DMA((4,)),
                pltpu.SemaphoreType.DMA((4, batch)),
                pltpu.SemaphoreType.DMA((4, groups - 1)),
                pltpu.SemaphoreType.DMA((4, groups - 1)),
                pltpu.SemaphoreType.DMA((rounds, groups)),
                pltpu.SemaphoreType.DMA((rounds, groups)),
            ],
            compiler_params=pltpu.CompilerParams(
                collective_id=0, has_side_effects=True, vmem_limit_bytes=44 * 1024 * 1024),
        )(*views, *flat, x_token, w_q, w_k, w_v, w_o, w_gate, w_up, w_down, norm_gain, qk_gain, rope)
        outs = [y.transpose(0, 1, 3, 2, 4).reshape(batch, y.shape[1], 2, head_dim) for y in res[:4]]
        return (res[4], *outs)

    return jax.shard_map(per_device, mesh=mesh, in_specs=(cache_in, cache_in, cache_in, cache_in, token_spec, col_split, col_split, col_split, row_split, col_split, col_split, row_split, replicated, replicated), out_specs=(token_spec, cache_out, cache_out, cache_out, cache_out), check_vma=False)
```

time: 398 us -> 165 us (0.41); the launches traced: 391 us -> 165 us
  Pallas kernels: 0 us -> 157 us
  blocking collectives: 91.5 us -> 0 us
  local copies, waits for them, and re-layouts: 87.2 us -> 7.53 us
  matrix products: 69.5 us -> 0 us
  other arithmetic: 56.1 us -> 0 us
  starting transfers between devices: 48.1 us -> 0 us
  waiting for transfers between devices: 36.4 us -> 0 us
    pallas_call x0 -> x1, Pallas kernels: none -> 157 us  [per_device(): pl.pallas_call(functools.partial(kernel, cfg), in_specs=[any_spec] * 19,...]
    psum x4 -> x0, blocking collectives: 91.5 us -> none  [the longest x2 48.5 us: finish_layer(): lax.psum(jnp.dot(gated_act, w_down[layer_idx], preferred_element_type=jnp...]
    dot_general x16 -> x0, matrix products: 69.5 us -> none  [the longest x2 28.7 us: finish_layer(): jnp.dot(gated_act, w_down[layer_idx], preferred_element_type=jnp.float32)]
    dot_general x11 -> x0, local copies, waits for them, and re-layouts: 46.4 us -> none  [the longest x3 15.8 us: project_qkv(): jnp.dot(normed, w_v[layer_idx], preferred_element_type=jnp.float32)]
    ppermute x16 -> x0, starting transfers between devices: 34.8 us -> none  [move_window(): incoming = lax.ppermute(outgoing, 'tp', send_pairs)]
    concatenate x5 -> x0, other arithmetic: 27.5 us -> none  [the longest x1 27.4 us: per_device(): v_cache = jnp.concatenate([moved_v, v_new[:, None], zero_slots], axis=1)]
    all_to_all x2 -> x0, waiting for transfers between devices: 26.3 us -> none  [the longest x1 26.3 us: per_device(): moved_v = lax.all_to_all(v_global, 'tp', 2, 1, tiled=True)]
    select_n x16 -> x0, other arithmetic: 25.3 us -> none  [move_window(): window_buf = jnp.where(recv_block < src_count, placed, window_buf)]
  transfers between devices with their start and end apart: 18 -> 0, of which waited for: 4 -> 0; matrix products, arithmetic and copies ran while one was open for 35% -> 0% of each run, Pallas kernels for 0% -> 0%
where the time goes in v1:
time: 165 us
  Pallas kernels  157 us (95%)
  local copies, waits for them, and re-layouts  7.53 us (5%)
    pallas_call x1, Pallas kernels, per_device(): pl.pallas_call(functools.partial(kernel, cfg), in_specs=[any_spec] * 19,...  157 us
    unnamed x7, local copies, waits for them, and re-layouts  7.53 us

profile of v1, /device:TPU:113, one launch (start us, length us, event | category | flops | bytes accessed | tf_op | source)
XLA Modules:
  0.0 165.1 jit_solution(11778341529317737655)
XLA Ops:
  0.6 157.0 %shard_map.182 = (bf16[3,1024,2,2,128]{4,3,2,1,0:T(2,128)(2,1)S(1)}, bf16[3,1024,2,2,128]{4,3,2,1,0:T(2,128)(2,1)S(1)}, bf16[3,1152,2,2,128]{4,3,2,1,0:T(2,128)(...) custom-call(bf16[3,128,2,2,4,2,128]{6,5,4,3,2,1,0:T(2,128)(2,1)} %bitcast.32, ...), custom_call_target="tpu_custom_call" | custom-call | tf_op jit(solution)/shard_map/pallas_call | solution.py:352
  157.6 1.7 %copy.25 = bf16[3,1024,2,256]{3,2,1,0:T(2,128)(2,1)} copy(bf16[3,1024,2,256]{3,2,1,0:T(2,128)(2,1)S(1)} %bitcast.31) | data formatting | bytes 6291456
  159.3 1.7 %copy.26 = bf16[3,1024,2,256]{3,2,1,0:T(2,128)(2,1)} copy(bf16[3,1024,2,256]{3,2,1,0:T(2,128)(2,1)S(1)} %bitcast.30) | data formatting | bytes 6291456
  160.9 1.8 %copy.27 = bf16[3,1152,2,256]{3,2,1,0:T(2,128)(2,1)} copy(bf16[3,1152,2,256]{3,2,1,0:T(2,128)(2,1)S(1)} %bitcast.29) | data formatting | bytes 7077888
  162.7 0.0 copy-start
  162.7 1.8 %copy.28 = bf16[3,1152,2,256]{3,2,1,0:T(2,128)(2,1)} copy(bf16[3,1152,2,256]{3,2,1,0:T(2,128)(2,1)S(1)} %bitcast.28) | data formatting | bytes 7077888
  164.5 0.0 copy-done
  164.5 0.6 copy.29
Async XLA Ops:
  162.7 1.8 %copy-start = (bf16[3,3072]{1,0:T(4,128)(2,1)S(1)}, bf16[3,3072]{1,0:T(4,128)(2,1)}, u32[]{:S(2)}) copy-start(bf16[3,3072]{1,0:T(4,128)(2,1)} %get-tuple-element.25) | copy-start | bytes 55300

commit v2 on v1

--- a/solution.py
+++ b/solution.py
@@ -17,12 +17,14 @@
 MESH = pl.DeviceIdType.MESH
 LANES = 128
 ROWS = 8
+TOKENS = 4
 RING = 8
 CHUNK = 512
-HALVES = 2
-FIRST_UNITS = 2
-ROUND_UNITS = (1, 1, 1, 1, 3, 1, 1)
-ROUNDS = len(ROUND_UNITS)
+SPLITS = 4
+FIRST_UNITS = 4
+ROUND_UNITS = (2, 2, 2, 2, 6, 2, 2, 2, 2, 2, 2, 6, 2, 2)
+ROUNDS = 7
+STEPS = 9
 
 
 def rms_norm(values, gain_vec):
@@ -37,7 +39,8 @@
     views, caches = ins[:4], ins[4:8]
     x_hbm, wq, wk, wv, wo, wg, wu, wd, ng_hbm, qk_hbm, rope_hbm = ins[8:]
     cache_out, h_out = outs[:4], outs[4]
-    (ring, wo_buf, kv, x_vm, ng, qkg, rope, h_ref, lhs, acc, q_all, st_all, o_all, part, rs_all, ag_all,
+    (ring, wo_buf, kv, x_vm, ng, qkg, rope, h_ref, lhs, acc, q_all, st_all, o_part, o_pair, o_sum, o_cross,
+     part, rs_pair, rs_sum, rs_cross, ag_all,
      ring_sem, wo_sem, kv_sem, small_sem, self_sem, bulk_send, bulk_recv, r_send, r_recv) = scr
     me = lax.axis_index("tp")
     per_tile = heads // 2
@@ -84,6 +87,9 @@
             return carry
         lax.fori_loop(0, count, step, 0)
 
+    barrier = pltpu.get_barrier_semaphore()
+    for k in range(1, groups):
+        pl.semaphore_signal(barrier, inc=1, device_id={"tp": (me + k) % groups}, device_id_type=MESH)
     small = [pltpu.make_async_copy(s, d, small_sem.at[n]) for n, (s, d) in enumerate(
         ((x_hbm, x_vm), (ng_hbm, ng), (qk_hbm, qkg), (rope_hbm, rope)))]
     for c in small:
@@ -98,13 +104,10 @@
     for n in range(3, RING):
         issue(n)
 
-    barrier = pltpu.get_barrier_semaphore()
-    for k in range(1, groups):
-        pl.semaphore_signal(barrier, inc=1, device_id={"tp": (me + k) % groups}, device_id_type=MESH)
     pl.semaphore_wait(barrier, groups - 1)
 
-    span = seq_dev // HALVES
-    units = [(c, b, f) for c in range(4) for b in range(batch) for f in range(HALVES)]
+    span = seq_dev // SPLITS
+    units = [(c, b, f) for c in range(4) for b in range(batch) for f in range(SPLITS)]
     chips = groups // 2
     order = [(dx, dc) for dc in range(2) for dx in (1, chips - 1, *range(2, chips - 1))] + [(0, 1)]
     chip, core = me // 2, me % 2
@@ -125,30 +128,58 @@
                 pltpu.make_async_remote_copy(
                     view_of(c, dst, b, f * span, span),
                     cache_out[c].at[b, pl.ds(me * seq_dev + f * span, span)],
-                    bulk_send.at[c, k], bulk_recv.at[c, k],
+                    bulk_send.at[c], bulk_recv.at[c],
                     device_id={"tp": dst}, device_id_type=MESH).start()
 
     bulk(FIRST_UNITS)
     self_copies = [pltpu.make_async_copy(
-        view_of(c, me, b, 0, seq_dev), cache_out[c].at[b, pl.ds(me * seq_dev, seq_dev)], self_sem.at[c, b])
+        view_of(c, me, b, 0, seq_dev), cache_out[c].at[b, pl.ds(me * seq_dev, seq_dev)], self_sem.at[c])
         for c in range(4) for b in range(batch)]
     for c in self_copies:
         c.start()
     kv_copies[2].start()
     kv_copies[3].start()
 
-    sent = []
-
-    def send(rnd, src_of, dst_ref):
-        got = []
-        for k in range(1, groups):
-            d = (me + k) % groups
-            c = pltpu.make_async_remote_copy(src_of(d), dst_ref.at[me], r_send.at[rnd, k], r_recv.at[rnd, k],
-                                             device_id={"tp": d}, device_id_type=MESH)
-            c.start()
-            got.append(c)
-        sent.extend(got)
-        return got
+    sibling = chip * 2 + 1 - core
+    pending = {}
+
+    def start_round(step, copies, size_of):
+        finish_sends(step)
+        for src, dst, device in copies:
+            pltpu.make_async_remote_copy(src, dst, r_send.at[step], r_recv.at[step],
+                                         device_id={"tp": device}, device_id_type=MESH).start()
+        pending[step] = pltpu.make_async_remote_copy(size_of, size_of, r_send.at[step], r_recv.at[step],
+                                                     device_id={"tp": sibling}, device_id_type=MESH)
+        return pending[step]
+
+    def finish_sends(step):
+        if step in pending:
+            pending.pop(step).wait_send()
+
+    others = [(chip + dx) % chips for dx in (1, chips - 1, *range(2, chips - 1))]
+
+    def gather_cross(step, ref, units):
+        got = start_round(step, [(ref.at[core, chip], ref.at[core, chip], t * 2 + core) for t in others],
+                          ref.at[core, pl.ds(0, chips - 1)])
+        bulk(units)
+        got.wait_recv()
+
+    def gather_pair(step, ref):
+        start_round(step, [(ref.at[core], ref.at[core], sibling)], ref.at[core]).wait_recv()
+
+    def scatter(step, mine, pair, summed, cross, units):
+        start_round(step, [(mine.at[1 - core], pair, sibling)], pair).wait_recv()
+        for t in range(chips):
+            summed[t] = mine[core, t] + pair[t]
+        got = start_round(step + 1, [(summed.at[t], cross.at[chip], t * 2 + core) for t in others],
+                          cross.at[pl.ds(0, chips - 1)])
+        bulk(units)
+        cross[chip] = summed[chip]
+        got.wait_recv()
+        total = cross[0]
+        for t in range(1, chips):
+            total = total + cross[t]
+        return total
 
     row = lax.broadcasted_iota(jnp.int32, (ROWS, LANES), 0)
     lane = lax.broadcasted_iota(jnp.int32, (ROWS, LANES), 1)
@@ -179,33 +210,30 @@
         a, b = x[:, :half_dim], x[:, half_dim:]
         return jnp.concatenate([a * cos - b * sin, b * cos + a * sin], axis=-1)
 
+    row1 = lax.broadcasted_iota(jnp.int32, (ROWS, 1), 0)
+
     def pick(y):
+        y = jnp.where(row1 == 0, y, jnp.where(row1 < 3, pltpu.roll(y, 1, 0), jnp.where(
+            row1 < 5, pltpu.roll(y, 2, 0), pltpu.roll(y, 3, 0))))
         return jnp.where(even, y[:, :head_dim], y[:, head_dim:])
 
-    def all_reduce(rnd, layer, slot):
-        got = send(rnd, lambda d: part.at[slot, d], rs_all.at[slot])
-        bulk(ROUND_UNITS[(rnd % ROUNDS)])
-        rs_all[slot, me] = part[slot, me]
-        for c in got:
-            c.wait_recv()
-        total = rs_all[slot, 0]
-        for s in range(1, groups):
-            total = total + rs_all[slot, s]
-        ag_all[slot, me] = total
-        got = send(rnd + 1, lambda d: ag_all.at[slot, me], ag_all.at[slot])
-        bulk(ROUND_UNITS[(rnd + 1) % ROUNDS])
-        for c in got:
-            c.wait_recv()
-        return jnp.concatenate([ag_all[slot, s] for s in range(groups)], axis=-1)
+    def merge(y):
+        y = y + pltpu.roll(y, ROWS - 1, 0)
+        return jnp.where(row1 == 0, y, jnp.where(row1 == 1, pltpu.roll(y, ROWS - 1, 0), jnp.where(
+            row1 == 2, pltpu.roll(y, ROWS - 2, 0), 0.0)))
+
+    def all_reduce(rnd, slot):
+        ag_all[slot, core, chip] = scatter(5, part.at[slot], rs_pair.at[slot], rs_sum.at[slot], rs_cross.at[slot],
+                                           ROUND_UNITS[rnd])
+        gather_cross(7, ag_all.at[slot], ROUND_UNITS[rnd + 1])
+        gather_pair(8, ag_all.at[slot])
+        whole = jnp.concatenate([ag_all[slot, s % 2, s // 2] for s in range(groups)], axis=-1)
+        return jnp.concatenate([whole, jnp.zeros((ROWS - TOKENS, width), jnp.float32)], axis=0)
 
     for c in small:
         c.wait()
-    x = x_vm[...].astype(jnp.float32)
-    wide8 = lax.broadcasted_iota(jnp.int32, (ROWS, width), 0) // 2
-    h0 = jnp.zeros((ROWS, width), jnp.float32)
-    for b in range(batch):
-        h0 = jnp.where(wide8 == b, jnp.broadcast_to(x[b:b + 1], (ROWS, width)), h0)
-    h_ref[...] = h0
+    h_ref[...] = jnp.concatenate(
+        [x_vm[...].astype(jnp.float32), jnp.zeros((ROWS - batch, width), jnp.float32)], axis=0)
 
     new_rows = []
     for layer in range(layers):
@@ -213,10 +241,11 @@
         base = layer * per_layer
         lhs[...] = rms_norm(h_ref[...], ng[layer, 0:1, :]).astype(jnp.bfloat16)
         stream(base, 3)
-        q = rope_rotate(rms_norm(pick(acc[0]), qkg[layer, 0:1, :]), layer).astype(jnp.bfloat16).astype(jnp.float32)
-        q_all[layer, me] = q
-        got = send(rnd, lambda d: q_all.at[layer, me], q_all.at[layer])
-        bulk(ROUND_UNITS[0])
+        q = rope_rotate(rms_norm(pick(acc[0]), qkg[layer, 0:1, :]), layer).astype(jnp.bfloat16)
+        q_all[layer, core, chip] = q
+        q = q.astype(jnp.float32)
+        gather_cross(0, q_all.at[layer], ROUND_UNITS[rnd])
+        gather_pair(1, q_all.at[layer])
         k_new = rope_rotate(rms_norm(pick(acc[1]), qkg[layer, 1:2, :]), layer).astype(jnp.bfloat16).astype(jnp.float32)
         v_new = pick(acc[2]).astype(jnp.bfloat16).astype(jnp.float32)
         new_rows.append((k_new, v_new))
@@ -224,9 +253,7 @@
         s_new = jnp.sum(q * k_new, axis=-1, keepdims=True) * scale
         kv_copies[2 * layer].wait()
         kv_copies[2 * layer + 1].wait()
-        for c in got:
-            c.wait_recv()
-        q64 = q_all[layer].reshape(groups * ROWS, head_dim).astype(jnp.bfloat16)
+        q64 = jnp.concatenate([q_all[layer, s % 2, s // 2].astype(jnp.float32) for s in range(groups)], axis=0).astype(jnp.bfloat16)
         scores = jnp.zeros((ROWS, seq_dev * heads), jnp.float32)
         for b in range(batch):
             s = lax.dot_general(q64, kv[2 * layer, b], (((1,), (1,)), ((), ())), preferred_element_type=jnp.float32)
@@ -242,15 +269,18 @@
         ex = jnp.where(valid, jnp.exp(scores - jnp.tile(m_loc, (1, col_tiles))), 0.0)
         l_loc = fold(ex, jnp.add)
         l_loc = jnp.where(own, l_loc + jnp.exp(s_new - m_loc), l_loc)
-        st_all[layer, me] = jnp.where(lane < LANES // 2, m_loc, l_loc)
-        got = send(rnd + 1, lambda d: st_all.at[layer, me], st_all.at[layer])
-        bulk(ROUND_UNITS[1])
-        for c in got:
-            c.wait_recv()
-        stats = [st_all[layer, s] for s in range(groups)]
-        low = lane < LANES // 2
-        ms = [jnp.where(low, t, pltpu.roll(t, LANES // 2, 1)) for t in stats]
-        ls = [jnp.where(low, pltpu.roll(t, LANES // 2, 1), t) for t in stats]
+        mine = lane // heads == row
+        st_all[layer, me] = jnp.concatenate(
+            [jnp.sum(jnp.where(mine, t, 0.0), axis=0, keepdims=True) for t in (m_loc, l_loc)], axis=0)
+        got = start_round(2, [(st_all.at[layer, me], st_all.at[layer, me], (me + k) % groups) for k in range(1, groups)],
+                          st_all.at[layer, pl.ds(0, groups - 1)])
+        bulk(ROUND_UNITS[rnd + 1])
+        got.wait_recv()
+        def unpack(s, n):
+            return fold(jnp.where(mine, jnp.broadcast_to(st_all[layer, s, n:n + 1, :], (ROWS, LANES)), 0.0), jnp.add)
+
+        ms = [unpack(s, 0) for s in range(groups)]
+        ls = [unpack(s, 1) for s in range(groups)]
         m_all = functools.reduce(jnp.maximum, ms)
         l_all = functools.reduce(jnp.add, [l * jnp.exp(m - m_all) for m, l in zip(ms, ls)])
         l_all = jnp.where(row < 2 * batch, jnp.maximum(l_all, 1e-30), 1.0)
@@ -258,29 +288,24 @@
         p_new = jnp.where(own & (lane < heads), jnp.exp(jnp.minimum(s_new - m_all, 0.0)) / l_all, 0.0)
         p_new = jnp.sum(p_new, axis=-1, keepdims=True).astype(jnp.bfloat16).astype(jnp.float32)
         prob64 = jnp.concatenate([prob] * groups, axis=0)
-        o_part = jnp.zeros((groups * ROWS, head_dim), jnp.float32)
+        weighted = jnp.zeros((groups * ROWS, head_dim), jnp.float32)
         for b in range(batch):
-            o_part = o_part + jnp.dot(jnp.where(hits[b], prob64, 0.0).astype(jnp.bfloat16), kv[2 * layer + 1, b],
-                                      preferred_element_type=jnp.float32)
-        o_all[layer, 0] = o_part.reshape(groups, ROWS, head_dim)
-        got = send(rnd + 2, lambda d: o_all.at[layer, 0, d], o_all.at[layer, 1])
-        bulk(ROUND_UNITS[2])
-        o_all[layer, 1, me] = o_all[layer, 0, me]
-        for c in got:
-            c.wait_recv()
-        o = p_new * v_new
-        for s in range(groups):
-            o = o + o_all[layer, 1, s]
+            weighted = weighted + jnp.dot(jnp.where(hits[b], prob64, 0.0).astype(jnp.bfloat16), kv[2 * layer + 1, b],
+                                          preferred_element_type=jnp.float32)
+        for d in range(groups):
+            o_part[layer, d % 2, d // 2] = weighted[d * ROWS:(d + 1) * ROWS]
+        o = scatter(3, o_part.at[layer], o_pair.at[layer], o_sum.at[layer], o_cross.at[layer], ROUND_UNITS[rnd + 2])
+        o = o + p_new * v_new
         o = o.astype(jnp.bfloat16).astype(jnp.float32)
         o = jnp.concatenate([jnp.where(even, o, 0.0), jnp.where(even, 0.0, o)], axis=-1).astype(jnp.bfloat16)
         wo_copies[layer].wait()
         piece = width // groups
         for d in range(groups):
             y = jnp.dot(o, wo_buf[:, d * piece:(d + 1) * piece], preferred_element_type=jnp.float32)
-            part[2 * layer, d] = y + jnp.where(even, pltpu.roll(y, ROWS - 1, 0), pltpu.roll(y, 1, 0))
+            part[2 * layer, d % 2, d // 2] = merge(y)[:TOKENS]
         if layer + 1 < layers:
             wo_copies[layer + 1].start()
-        hidden = h_ref[...] + rms_norm(all_reduce(rnd + 3, layer, 2 * layer), ng[layer, 1:2, :])
+        hidden = h_ref[...] + rms_norm(all_reduce(rnd + 3, 2 * layer), ng[layer, 1:2, :])
         h_ref[...] = hidden
         lhs[...] = rms_norm(hidden, ng[layer, 2:3, :]).astype(jnp.bfloat16)
         stream(base + 3, 2 * ff_items)
@@ -290,29 +315,27 @@
         stream(base + 3 + 2 * ff_items, wd_items)
         full = jnp.concatenate([acc[n] for n in range(wd_items)], axis=-1)
         for d in range(groups):
-            part[2 * layer + 1, d] = full[:, d * piece:(d + 1) * piece]
-        hidden = h_ref[...] + rms_norm(all_reduce(rnd + 5, layer, 2 * layer + 1), ng[layer, 3:4, :])
+            part[2 * layer + 1, d % 2, d // 2] = full[:TOKENS, d * piece:(d + 1) * piece]
+        hidden = h_ref[...] + rms_norm(all_reduce(rnd + 5, 2 * layer + 1), ng[layer, 3:4, :])
         h_ref[...] = hidden.astype(jnp.bfloat16).astype(jnp.float32)
 
     bulk(len(queue))
     for b in range(batch):
-        h_out[b:b + 1, :] = h_ref[2 * b:2 * b + 1, :].astype(jnp.bfloat16)
+        h_out[b:b + 1, :] = h_ref[b:b + 1, :].astype(jnp.bfloat16)
     zeros = jnp.zeros((NEW_SLOTS - 1, 2, 2, LANES), jnp.bfloat16)
     for c in (2, 3):
         for b in range(batch):
             cache_out[c][b, seq + 1:] = zeros
-    for c in sent:
-        c.wait_send()
-    for c in self_copies:
-        c.wait()
+    for step in list(pending):
+        finish_sends(step)
     for c in range(4):
-        for k, (dx, dc) in enumerate(order):
-            src = peer(-dx % chips, dc)
-            region = cache_out[c].at[0:batch, pl.ds(src * seq_dev, seq_dev)]
-            whole = pltpu.make_async_remote_copy(region, region, bulk_send.at[c, k], bulk_recv.at[c, k],
-                                                 device_id={"tp": peer(dx, dc)}, device_id_type=MESH)
-            whole.wait_recv()
-            whole.wait_send()
+        own_rows = cache_out[c].at[0:batch, pl.ds(me * seq_dev, seq_dev)]
+        pltpu.make_async_copy(own_rows, own_rows, self_sem.at[c]).wait()
+        region = cache_out[c].at[0:batch, pl.ds(0, seq - seq_dev)]
+        whole = pltpu.make_async_remote_copy(region, region, bulk_send.at[c], bulk_recv.at[c],
+                                             device_id={"tp": sibling}, device_id_type=MESH)
+        whole.wait_recv()
+        whole.wait_send()
     slots = (seq % WINDOW, seq)
     for layer in range(layers):
         for n in range(2):
@@ -320,6 +343,15 @@
                 for ct in range(2):
                     cache_out[2 * layer + n][b, slots[layer], ct] = new_rows[layer][n][
                         2 * b:2 * b + 2, ct * LANES:(ct + 1) * LANES].astype(jnp.bfloat16)
+
+
+def flush_kernel(*refs):
+    n = (len(refs) - 1) // 2
+    copies = [pltpu.make_async_copy(refs[i], refs[n + i], refs[-1].at[i]) for i in range(n)]
+    for c in copies:
+        c.start()
+    for c in copies:
+        c.wait()
 
 
 def solution(mesh):
@@ -348,13 +380,13 @@
         cfg = (groups, layers, batch, seq_dev, heads, head_dim, width, ff_dev)
         slots = (WINDOW, WINDOW, seq + NEW_SLOTS, seq + NEW_SLOTS)
         piece = width // groups
-        rounds = layers * ROUNDS
+        chips = groups // 2
         res = pl.pallas_call(
             functools.partial(kernel, cfg),
             in_specs=[any_spec] * 19,
             out_specs=[vmem_spec] * 5,
             out_shape=[pltpu.VMEM((batch, s, 2, 2, LANES), jnp.bfloat16) for s in slots]
-            + [jax.ShapeDtypeStruct((batch, width), jnp.bfloat16)],
+            + [pltpu.VMEM((batch, width), jnp.bfloat16)],
             scratch_shapes=[
                 pltpu.VMEM((RING, width, CHUNK), jnp.bfloat16),
                 pltpu.VMEM((w_o.shape[1], width), jnp.bfloat16),
@@ -366,25 +398,35 @@
                 pltpu.VMEM((ROWS, width), jnp.float32),
                 pltpu.VMEM((ROWS, width), jnp.bfloat16),
                 pltpu.VMEM((2 * ff_dev // CHUNK, ROWS, CHUNK), jnp.float32),
-                pltpu.VMEM((layers, groups, ROWS, head_dim), jnp.float32),
-                pltpu.VMEM((layers, groups, ROWS, LANES), jnp.float32),
-                pltpu.VMEM((layers, 2, groups, ROWS, head_dim), jnp.float32),
-                pltpu.VMEM((2 * layers, groups, ROWS, piece), jnp.float32),
-                pltpu.VMEM((2 * layers, groups, ROWS, piece), jnp.float32),
-                pltpu.VMEM((2 * layers, groups, ROWS, piece), jnp.float32),
+                pltpu.VMEM((layers, 2, chips, ROWS, head_dim), jnp.bfloat16),
+                pltpu.VMEM((layers, groups, 2, LANES), jnp.float32),
+                pltpu.VMEM((layers, 2, chips, ROWS, head_dim), jnp.float32),
+                *[pltpu.VMEM((layers, chips, ROWS, head_dim), jnp.float32)] * 3,
+                pltpu.VMEM((2 * layers, 2, chips, TOKENS, piece), jnp.float32),
+                *[pltpu.VMEM((2 * layers, chips, TOKENS, piece), jnp.float32)] * 3,
+                pltpu.VMEM((2 * layers, 2, chips, TOKENS, piece), jnp.float32),
                 pltpu.SemaphoreType.DMA((RING,)),
                 pltpu.SemaphoreType.DMA((layers,)),
                 pltpu.SemaphoreType.DMA((4,)),
                 pltpu.SemaphoreType.DMA((4,)),
-                pltpu.SemaphoreType.DMA((4, batch)),
-                pltpu.SemaphoreType.DMA((4, groups - 1)),
-                pltpu.SemaphoreType.DMA((4, groups - 1)),
-                pltpu.SemaphoreType.DMA((rounds, groups)),
-                pltpu.SemaphoreType.DMA((rounds, groups)),
+                pltpu.SemaphoreType.DMA((4,)),
+                pltpu.SemaphoreType.DMA((4,)),
+                pltpu.SemaphoreType.DMA((4,)),
+                pltpu.SemaphoreType.DMA((STEPS,)),
+                pltpu.SemaphoreType.DMA((STEPS,)),
             ],
             compiler_params=pltpu.CompilerParams(
                 collective_id=0, has_side_effects=True, vmem_limit_bytes=44 * 1024 * 1024),
         )(*views, *flat, x_token, w_q, w_k, w_v, w_o, w_gate, w_up, w_down, norm_gain, qk_gain, rope)
+        held = [pltpu.with_memory_space_constraint(y, pltpu.VMEM) for y in res]
+        res = pl.pallas_call(
+            flush_kernel,
+            in_specs=[vmem_spec] * 5,
+            out_specs=[any_spec] * 5,
+            out_shape=[jax.ShapeDtypeStruct(y.shape, y.dtype) for y in res],
+            scratch_shapes=[pltpu.SemaphoreType.DMA((5,))],
+            compiler_params=pltpu.CompilerParams(has_side_effects=True, vmem_limit_bytes=1024 * 1024),
+        )(*held)
         outs = [y.transpose(0, 1, 3, 2, 4).reshape(batch, y.shape[1], 2, head_dim) for y in res[:4]]
         return (res[4], *outs)
 

time: 165 us -> 151 us (0.915)
  local copies, waits for them, and re-layouts: 7.53 us -> 0 us
  Pallas kernels: 157 us -> 151 us
    pallas_call x1, Pallas kernels: 157 us -> 146 us  [per_device(): pl.pallas_call(functools.partial(kernel, cfg), in_specs=[any_spec] * 19,...]
    unnamed x7 -> x0, local copies, waits for them, and re-layouts: 7.53 us -> none
    pallas_call x0 -> x1, Pallas kernels: none -> 4.98 us  [per_device(): pl.pallas_call(flush_kernel, in_specs=[vmem_spec] * 5, out_specs=[any_spe...]
where the time goes in v2:
time: 151 us
  Pallas kernels  151 us (100%)
    pallas_call x1, Pallas kernels, per_device(): pl.pallas_call(functools.partial(kernel, cfg), in_specs=[any_spec] * 19,...  146 us
    pallas_call x1, Pallas kernels, per_device(): pl.pallas_call(flush_kernel, in_specs=[vmem_spec] * 5, out_specs=[any_spe...  4.98 us

profile of v2, /device:TPU:113, one launch (start us, length us, event | category | flops | bytes accessed | tf_op | source)
XLA Modules:
  0.0 151.2 jit_solution(835623902217393925)
XLA Ops:
  0.6 145.6 %shard_map.182 = (bf16[3,1024,2,2,128]{4,3,2,1,0:T(2,128)(2,1)S(1)}, bf16[3,1024,2,2,128]{4,3,2,1,0:T(2,128)(2,1)S(1)}, bf16[3,1152,2,2,128]{4,3,2,1,0:T(2,128)(...) custom-call(bf16[3,128,2,2,4,2,128]{6,5,4,3,2,1,0:T(2,128)(2,1)} %bitcast.28, ...), custom_call_target="tpu_custom_call" | custom-call | tf_op jit(solution)/shard_map/pallas_call | solution.py:384
  146.2 5.0 %shard_map.183 = (bf16[3,1024,2,2,128]{4,3,2,1,0:T(2,128)(2,1)}, bf16[3,1024,2,2,128]{4,3,2,1,0:T(2,128)(2,1)}, bf16[3,1152,2,2,128]{4,3,2,1,0:T(2,128)(2,1)}, b...) custom-call(bf16[3,1024,2,2,128]{4,3,2,1,0:T(2,128)(2,1)S(1)} %get-tuple-element.15.refs_0_, ...), custom_call_target="tpu_custom_call" | custom-call | tf_op jit(solution)/shard_map/pallas_call | solution.py:422

commit v3 on v2

--- a/solution.py
+++ b/solution.py
@@ -17,7 +17,6 @@
 MESH = pl.DeviceIdType.MESH
 LANES = 128
 ROWS = 8
-TOKENS = 4
 RING = 8
 CHUNK = 512
 SPLITS = 4
@@ -217,6 +216,9 @@
             row1 < 5, pltpu.roll(y, 2, 0), pltpu.roll(y, 3, 0))))
         return jnp.where(even, y[:, :head_dim], y[:, head_dim:])
 
+    def pair_rows(y):
+        return jnp.concatenate([*(y[b] for b in range(batch)), jnp.zeros((ROWS - 2 * batch, head_dim), jnp.float32)], axis=0)
+
     def merge(y):
         y = y + pltpu.roll(y, ROWS - 1, 0)
         return jnp.where(row1 == 0, y, jnp.where(row1 == 1, pltpu.roll(y, ROWS - 1, 0), jnp.where(
@@ -227,8 +229,8 @@
                                            ROUND_UNITS[rnd])
         gather_cross(7, ag_all.at[slot], ROUND_UNITS[rnd + 1])
         gather_pair(8, ag_all.at[slot])
-        whole = jnp.concatenate([ag_all[slot, s % 2, s // 2] for s in range(groups)], axis=-1)
-        return jnp.concatenate([whole, jnp.zeros((ROWS - TOKENS, width), jnp.float32)], axis=0)
+        whole = [jnp.concatenate([ag_all[slot, s % 2, s // 2, b] for s in range(groups)], axis=-1) for b in range(batch)]
+        return jnp.concatenate([*whole, jnp.zeros((ROWS - batch, width), jnp.float32)], axis=0)
 
     for c in small:
         c.wait()
@@ -241,9 +243,9 @@
         base = layer * per_layer
         lhs[...] = rms_norm(h_ref[...], ng[layer, 0:1, :]).astype(jnp.bfloat16)
         stream(base, 3)
-        q = rope_rotate(rms_norm(pick(acc[0]), qkg[layer, 0:1, :]), layer).astype(jnp.bfloat16)
-        q_all[layer, core, chip] = q
-        q = q.astype(jnp.float32)
+        q = rope_rotate(rms_norm(pick(acc[0]), qkg[layer, 0:1, :]), layer).astype(jnp.bfloat16).astype(jnp.float32)
+        for b in range(batch):
+            q_all[layer, core, chip, b] = q[2 * b:2 * b + 2].astype(jnp.bfloat16)
         gather_cross(0, q_all.at[layer], ROUND_UNITS[rnd])
         gather_pair(1, q_all.at[layer])
         k_new = rope_rotate(rms_norm(pick(acc[1]), qkg[layer, 1:2, :]), layer).astype(jnp.bfloat16).astype(jnp.float32)
@@ -253,7 +255,7 @@
         s_new = jnp.sum(q * k_new, axis=-1, keepdims=True) * scale
         kv_copies[2 * layer].wait()
         kv_copies[2 * layer + 1].wait()
-        q64 = jnp.concatenate([q_all[layer, s % 2, s // 2].astype(jnp.float32) for s in range(groups)], axis=0).astype(jnp.bfloat16)
+        q64 = jnp.concatenate([pair_rows(q_all[layer, s % 2, s // 2].astype(jnp.float32)) for s in range(groups)], axis=0).astype(jnp.bfloat16)
         scores = jnp.zeros((ROWS, seq_dev * heads), jnp.float32)
         for b in range(batch):
             s = lax.dot_general(q64, kv[2 * layer, b], (((1,), (1,)), ((), ())), preferred_element_type=jnp.float32)
@@ -293,16 +295,19 @@
             weighted = weighted + jnp.dot(jnp.where(hits[b], prob64, 0.0).astype(jnp.bfloat16), kv[2 * layer + 1, b],
                                           preferred_element_type=jnp.float32)
         for d in range(groups):
-            o_part[layer, d % 2, d // 2] = weighted[d * ROWS:(d + 1) * ROWS]
+            for b in range(batch):
+                o_part[layer, d % 2, d // 2, b] = weighted[d * ROWS + 2 * b:d * ROWS + 2 * b + 2]
         o = scatter(3, o_part.at[layer], o_pair.at[layer], o_sum.at[layer], o_cross.at[layer], ROUND_UNITS[rnd + 2])
-        o = o + p_new * v_new
+        o = pair_rows(o) + p_new * v_new
         o = o.astype(jnp.bfloat16).astype(jnp.float32)
         o = jnp.concatenate([jnp.where(even, o, 0.0), jnp.where(even, 0.0, o)], axis=-1).astype(jnp.bfloat16)
         wo_copies[layer].wait()
         piece = width // groups
         for d in range(groups):
             y = jnp.dot(o, wo_buf[:, d * piece:(d + 1) * piece], preferred_element_type=jnp.float32)
-            part[2 * layer, d % 2, d // 2] = merge(y)[:TOKENS]
+            y = merge(y)
+            for b in range(batch):
+                part[2 * layer, d % 2, d // 2, b] = y[b:b + 1]
         if layer + 1 < layers:
             wo_copies[layer + 1].start()
         hidden = h_ref[...] + rms_norm(all_reduce(rnd + 3, 2 * layer), ng[layer, 1:2, :])
@@ -315,7 +320,8 @@
         stream(base + 3 + 2 * ff_items, wd_items)
         full = jnp.concatenate([acc[n] for n in range(wd_items)], axis=-1)
         for d in range(groups):
-            part[2 * layer + 1, d % 2, d // 2] = full[:TOKENS, d * piece:(d + 1) * piece]
+            for b in range(batch):
+                part[2 * layer + 1, d % 2, d // 2, b] = full[b:b + 1, d * piece:(d + 1) * piece]
         hidden = h_ref[...] + rms_norm(all_reduce(rnd + 5, 2 * layer + 1), ng[layer, 3:4, :])
         h_ref[...] = hidden.astype(jnp.bfloat16).astype(jnp.float32)
 
@@ -398,13 +404,13 @@
                 pltpu.VMEM((ROWS, width), jnp.float32),
                 pltpu.VMEM((ROWS, width), jnp.bfloat16),
                 pltpu.VMEM((2 * ff_dev // CHUNK, ROWS, CHUNK), jnp.float32),
-                pltpu.VMEM((layers, 2, chips, ROWS, head_dim), jnp.bfloat16),
+                pltpu.VMEM((layers, 2, chips, batch, 2, head_dim), jnp.bfloat16),
                 pltpu.VMEM((layers, groups, 2, LANES), jnp.float32),
-                pltpu.VMEM((layers, 2, chips, ROWS, head_dim), jnp.float32),
-                *[pltpu.VMEM((layers, chips, ROWS, head_dim), jnp.float32)] * 3,
-                pltpu.VMEM((2 * layers, 2, chips, TOKENS, piece), jnp.float32),
-                *[pltpu.VMEM((2 * layers, chips, TOKENS, piece), jnp.float32)] * 3,
-                pltpu.VMEM((2 * layers, 2, chips, TOKENS, piece), jnp.float32),
+                pltpu.VMEM((layers, 2, chips, batch, 2, head_dim), jnp.float32),
+                *[pltpu.VMEM((layers, chips, batch, 2, head_dim), jnp.float32)] * 3,
+                pltpu.VMEM((2 * layers, 2, chips, batch, 1, piece), jnp.float32),
+                *[pltpu.VMEM((2 * layers, chips, batch, 1, piece), jnp.float32)] * 3,
+                pltpu.VMEM((2 * layers, 2, chips, batch, 1, piece), jnp.float32),
                 pltpu.SemaphoreType.DMA((RING,)),
                 pltpu.SemaphoreType.DMA((layers,)),
                 pltpu.SemaphoreType.DMA((4,)),

time: 151 us -> 151 us (level)
  no operation moved by 1% of the time
where the time goes in v3:
time: 151 us
  Pallas kernels  150 us (99%)
    pallas_call x1, Pallas kernels, per_device(): pl.pallas_call(functools.partial(kernel, cfg), in_specs=[any_spec] * 19,...  145 us
    pallas_call x1, Pallas kernels, per_device(): pl.pallas_call(flush_kernel, in_specs=[vmem_spec] * 5, out_specs=[any_spe...  4.98 us

profile of v3, /device:TPU:113, one launch (start us, length us, event | category | flops | bytes accessed | tf_op | source)
XLA Modules:
  0.0 150.5 jit_solution(13022926812662275950)
XLA Ops:
  0.6 144.9 %shard_map.182 = (bf16[3,1024,2,2,128]{4,3,2,1,0:T(2,128)(2,1)S(1)}, bf16[3,1024,2,2,128]{4,3,2,1,0:T(2,128)(2,1)S(1)}, bf16[3,1152,2,2,128]{4,3,2,1,0:T(2,128)(...) custom-call(bf16[3,128,2,2,4,2,128]{6,5,4,3,2,1,0:T(2,128)(2,1)} %bitcast.28, ...), custom_call_target="tpu_custom_call" | custom-call | tf_op jit(solution)/shard_map/pallas_call | solution.py:390
  145.6 5.0 %shard_map.183 = (bf16[3,1024,2,2,128]{4,3,2,1,0:T(2,128)(2,1)}, bf16[3,1024,2,2,128]{4,3,2,1,0:T(2,128)(2,1)}, bf16[3,1152,2,2,128]{4,3,2,1,0:T(2,128)(2,1)}, b...) custom-call(bf16[3,1024,2,2,128]{4,3,2,1,0:T(2,128)(2,1)S(1)} %get-tuple-element.15.refs_0_, ...), custom_call_target="tpu_custom_call" | custom-call | tf_op jit(solution)/shard_map/pallas_call | solution.py:428

commit v4 on v3

--- a/solution.py
+++ b/solution.py
@@ -20,10 +20,9 @@
 RING = 8
 CHUNK = 512
 SPLITS = 4
-FIRST_UNITS = 4
+FIRST_UNITS = 6
 ROUND_UNITS = (2, 2, 2, 2, 6, 2, 2, 2, 2, 2, 2, 6, 2, 2)
 ROUNDS = 7
-STEPS = 9
 
 
 def rms_norm(values, gain_vec):
@@ -40,7 +39,7 @@
     cache_out, h_out = outs[:4], outs[4]
     (ring, wo_buf, kv, x_vm, ng, qkg, rope, h_ref, lhs, acc, q_all, st_all, o_part, o_pair, o_sum, o_cross,
      part, rs_pair, rs_sum, rs_cross, ag_all,
-     ring_sem, wo_sem, kv_sem, small_sem, self_sem, bulk_send, bulk_recv, r_send, r_recv) = scr
+     ring_sem, local_sem, bulk_sem, r_send, r_recv) = scr
     me = lax.axis_index("tp")
     per_tile = heads // 2
     pairs = per_tile // 2
@@ -52,7 +51,6 @@
     items = layers * per_layer
 
     def issue(item):
-        item = jnp.asarray(item, jnp.int32)
         layer = item // per_layer
         r = item % per_layer
         slot = item % RING
@@ -89,20 +87,6 @@
     barrier = pltpu.get_barrier_semaphore()
     for k in range(1, groups):
         pl.semaphore_signal(barrier, inc=1, device_id={"tp": (me + k) % groups}, device_id_type=MESH)
-    small = [pltpu.make_async_copy(s, d, small_sem.at[n]) for n, (s, d) in enumerate(
-        ((x_hbm, x_vm), (ng_hbm, ng), (qk_hbm, qkg), (rope_hbm, rope)))]
-    for c in small:
-        c.start()
-    for n in range(3):
-        issue(n)
-    kv_copies = [pltpu.make_async_copy(caches[n], kv.at[n], kv_sem.at[n]) for n in range(4)]
-    wo_copies = [pltpu.make_async_copy(wo.at[n], wo_buf, wo_sem.at[n]) for n in range(layers)]
-    kv_copies[0].start()
-    kv_copies[1].start()
-    wo_copies[0].start()
-    for n in range(3, RING):
-        issue(n)
-
     pl.semaphore_wait(barrier, groups - 1)
 
     span = seq_dev // SPLITS
@@ -127,50 +111,62 @@
                 pltpu.make_async_remote_copy(
                     view_of(c, dst, b, f * span, span),
                     cache_out[c].at[b, pl.ds(me * seq_dev + f * span, span)],
-                    bulk_send.at[c], bulk_recv.at[c],
+                    bulk_sem.at[0], bulk_sem.at[1],
                     device_id={"tp": dst}, device_id_type=MESH).start()
 
     bulk(FIRST_UNITS)
-    self_copies = [pltpu.make_async_copy(
-        view_of(c, me, b, 0, seq_dev), cache_out[c].at[b, pl.ds(me * seq_dev, seq_dev)], self_sem.at[c])
-        for c in range(4) for b in range(batch)]
-    for c in self_copies:
+    def load(src, dst, which):
+        c = pltpu.make_async_copy(src, dst, local_sem.at[which])
         c.start()
-    kv_copies[2].start()
-    kv_copies[3].start()
+        return c
+
+    SMALL, OUT, HEADS, SELF = range(4)
+    small = ((x_hbm, x_vm), (ng_hbm, ng), (qk_hbm, qkg), (rope_hbm, rope))
+    small_copies = [load(*small[0], SMALL)] + [load(*small[n], 3 + n) for n in (1, 2, 3)]
+    for n in range(3):
+        pltpu.make_async_copy((wq, wk, wv)[n].at[0], ring.at[n], ring_sem.at[n]).start()
+    load(caches[0], kv.at[0], HEADS)
+    load(caches[1], kv.at[1], HEADS)
+    wo_copy = load(wo.at[0], wo_buf, OUT)
+    for n in range(3, RING):
+        issue(jnp.int32(n))
+    for c in range(4):
+        for b in range(batch):
+            load(view_of(c, me, b, 0, seq_dev), cache_out[c].at[b, pl.ds(me * seq_dev, seq_dev)], SELF)
 
     sibling = chip * 2 + 1 - core
-    pending = {}
-
-    def start_round(step, copies, size_of):
-        finish_sends(step)
+    turns = {"pair": 0, "cross": 0, "all": 0}
+    pending = []
+
+    def start_round(kind, copies, size_of):
+        if len(pending) == 2:
+            pending.pop(0).wait_send()
+        turn = turns[kind]
+        turns[kind] += 1
+        s_sem = r_send.at[sum(turns.values()) % 2]
+        r_sem = r_recv.at[{"pair": 0, "cross": 2, "all": 4}[kind] + (turn % 2 if kind != "all" else 0)]
         for src, dst, device in copies:
-            pltpu.make_async_remote_copy(src, dst, r_send.at[step], r_recv.at[step],
-                                         device_id={"tp": device}, device_id_type=MESH).start()
-        pending[step] = pltpu.make_async_remote_copy(size_of, size_of, r_send.at[step], r_recv.at[step],
-                                                     device_id={"tp": sibling}, device_id_type=MESH)
-        return pending[step]
-
-    def finish_sends(step):
-        if step in pending:
-            pending.pop(step).wait_send()
+            pltpu.make_async_remote_copy(src, dst, s_sem, r_sem, device_id={"tp": device}, device_id_type=MESH).start()
+        pending.append(pltpu.make_async_remote_copy(size_of, size_of, s_sem, r_sem,
+                                                    device_id={"tp": sibling}, device_id_type=MESH))
+        return pending[-1]
 
     others = [(chip + dx) % chips for dx in (1, chips - 1, *range(2, chips - 1))]
 
-    def gather_cross(step, ref, units):
-        got = start_round(step, [(ref.at[core, chip], ref.at[core, chip], t * 2 + core) for t in others],
+    def gather_cross(ref, units):
+        got = start_round("cross", [(ref.at[core, chip], ref.at[core, chip], t * 2 + core) for t in others],
                           ref.at[core, pl.ds(0, chips - 1)])
         bulk(units)
         got.wait_recv()
 
-    def gather_pair(step, ref):
-        start_round(step, [(ref.at[core], ref.at[core], sibling)], ref.at[core]).wait_recv()
-
-    def scatter(step, mine, pair, summed, cross, units):
-        start_round(step, [(mine.at[1 - core], pair, sibling)], pair).wait_recv()
+    def gather_pair(ref):
+        start_round("pair", [(ref.at[core], ref.at[core], sibling)], ref.at[core]).wait_recv()
+
+    def scatter(mine, pair, summed, cross, units):
+        start_round("pair", [(mine.at[1 - core], pair, sibling)], pair).wait_recv()
         for t in range(chips):
             summed[t] = mine[core, t] + pair[t]
-        got = start_round(step + 1, [(summed.at[t], cross.at[chip], t * 2 + core) for t in others],
+        got = start_round("cross", [(summed.at[t], cross.at[chip], t * 2 + core) for t in others],
                           cross.at[pl.ds(0, chips - 1)])
         bulk(units)
         cross[chip] = summed[chip]
@@ -225,14 +221,14 @@
             row1 == 2, pltpu.roll(y, ROWS - 2, 0), 0.0)))
 
     def all_reduce(rnd, slot):
-        ag_all[slot, core, chip] = scatter(5, part.at[slot], rs_pair.at[slot], rs_sum.at[slot], rs_cross.at[slot],
+        ag_all[slot, core, chip] = scatter(part.at[slot], rs_pair.at[slot], rs_sum.at[slot], rs_cross.at[slot],
                                            ROUND_UNITS[rnd])
-        gather_cross(7, ag_all.at[slot], ROUND_UNITS[rnd + 1])
-        gather_pair(8, ag_all.at[slot])
+        gather_cross(ag_all.at[slot], ROUND_UNITS[rnd + 1])
+        gather_pair(ag_all.at[slot])
         whole = [jnp.concatenate([ag_all[slot, s % 2, s // 2, b] for s in range(groups)], axis=-1) for b in range(batch)]
         return jnp.concatenate([*whole, jnp.zeros((ROWS - batch, width), jnp.float32)], axis=0)
 
-    for c in small:
+    for c in small_copies:
         c.wait()
     h_ref[...] = jnp.concatenate(
         [x_vm[...].astype(jnp.float32), jnp.zeros((ROWS - batch, width), jnp.float32)], axis=0)
@@ -246,15 +242,18 @@
         q = rope_rotate(rms_norm(pick(acc[0]), qkg[layer, 0:1, :]), layer).astype(jnp.bfloat16).astype(jnp.float32)
         for b in range(batch):
             q_all[layer, core, chip, b] = q[2 * b:2 * b + 2].astype(jnp.bfloat16)
-        gather_cross(0, q_all.at[layer], ROUND_UNITS[rnd])
-        gather_pair(1, q_all.at[layer])
+        gather_cross(q_all.at[layer], ROUND_UNITS[rnd])
+        gather_pair(q_all.at[layer])
         k_new = rope_rotate(rms_norm(pick(acc[1]), qkg[layer, 1:2, :]), layer).astype(jnp.bfloat16).astype(jnp.float32)
         v_new = pick(acc[2]).astype(jnp.bfloat16).astype(jnp.float32)
         new_rows.append((k_new, v_new))
         scale = head_dim ** -0.5
         s_new = jnp.sum(q * k_new, axis=-1, keepdims=True) * scale
-        kv_copies[2 * layer].wait()
-        kv_copies[2 * layer + 1].wait()
+        both = kv.at[2 * layer:2 * layer + 2]
+        pltpu.make_async_copy(both, both, local_sem.at[HEADS]).wait()
+        if layer + 1 < layers:
+            load(caches[2 * layer + 2], kv.at[2 * layer + 2], HEADS)
+            load(caches[2 * layer + 3], kv.at[2 * layer + 3], HEADS)
         q64 = jnp.concatenate([pair_rows(q_all[layer, s % 2, s // 2].astype(jnp.float32)) for s in range(groups)], axis=0).astype(jnp.bfloat16)
         scores = jnp.zeros((ROWS, seq_dev * heads), jnp.float32)
         for b in range(batch):
@@ -274,7 +273,7 @@
         mine = lane // heads == row
         st_all[layer, me] = jnp.concatenate(
             [jnp.sum(jnp.where(mine, t, 0.0), axis=0, keepdims=True) for t in (m_loc, l_loc)], axis=0)
-        got = start_round(2, [(st_all.at[layer, me], st_all.at[layer, me], (me + k) % groups) for k in range(1, groups)],
+        got = start_round("all", [(st_all.at[layer, me], st_all.at[layer, me], (me + k) % groups) for k in range(1, groups)],
                           st_all.at[layer, pl.ds(0, groups - 1)])
         bulk(ROUND_UNITS[rnd + 1])
         got.wait_recv()
@@ -297,11 +296,11 @@
         for d in range(groups):
             for b in range(batch):
                 o_part[layer, d % 2, d // 2, b] = weighted[d * ROWS + 2 * b:d * ROWS + 2 * b + 2]
-        o = scatter(3, o_part.at[layer], o_pair.at[layer], o_sum.at[layer], o_cross.at[layer], ROUND_UNITS[rnd + 2])
+        o = scatter(o_part.at[layer], o_pair.at[layer], o_sum.at[layer], o_cross.at[layer], ROUND_UNITS[rnd + 2])
         o = pair_rows(o) + p_new * v_new
         o = o.astype(jnp.bfloat16).astype(jnp.float32)
         o = jnp.concatenate([jnp.where(even, o, 0.0), jnp.where(even, 0.0, o)], axis=-1).astype(jnp.bfloat16)
-        wo_copies[layer].wait()
+        wo_copy.wait()
         piece = width // groups
         for d in range(groups):
             y = jnp.dot(o, wo_buf[:, d * piece:(d + 1) * piece], preferred_element_type=jnp.float32)
@@ -309,7 +308,7 @@
             for b in range(batch):
                 part[2 * layer, d % 2, d // 2, b] = y[b:b + 1]
         if layer + 1 < layers:
-            wo_copies[layer + 1].start()
+            wo_copy = load(wo.at[layer + 1], wo_buf, OUT)
         hidden = h_ref[...] + rms_norm(all_reduce(rnd + 3, 2 * layer), ng[layer, 1:2, :])
         h_ref[...] = hidden
         lhs[...] = rms_norm(hidden, ng[layer, 2:3, :]).astype(jnp.bfloat16)
@@ -332,23 +331,26 @@
     for c in (2, 3):
         for b in range(batch):
             cache_out[c][b, seq + 1:] = zeros
-    for step in list(pending):
-        finish_sends(step)
-    for c in range(4):
-        own_rows = cache_out[c].at[0:batch, pl.ds(me * seq_dev, seq_dev)]
-        pltpu.make_async_copy(own_rows, own_rows, self_sem.at[c]).wait()
-        region = cache_out[c].at[0:batch, pl.ds(0, seq - seq_dev)]
-        whole = pltpu.make_async_remote_copy(region, region, bulk_send.at[c], bulk_recv.at[c],
-                                             device_id={"tp": sibling}, device_id_type=MESH)
-        whole.wait_recv()
-        whole.wait_send()
-    slots = (seq % WINDOW, seq)
-    for layer in range(layers):
-        for n in range(2):
-            for b in range(batch):
-                for ct in range(2):
-                    cache_out[2 * layer + n][b, slots[layer], ct] = new_rows[layer][n][
-                        2 * b:2 * b + 2, ct * LANES:(ct + 1) * LANES].astype(jnp.bfloat16)
+
+    def store_new(c):
+        for b in range(batch):
+            for ct in range(2):
+                cache_out[c][b, (seq % WINDOW, seq)[c // 2], ct] = new_rows[c // 2][c % 2][
+                    2 * b:2 * b + 2, ct * LANES:(ct + 1) * LANES].astype(jnp.bfloat16)
+
+    store_new(2)
+    store_new(3)
+    for c in pending:
+        c.wait_send()
+    own_rows = cache_out[0].at[0:batch, pl.ds(0, 4 * seq_dev)]
+    pltpu.make_async_copy(own_rows, own_rows, local_sem.at[SELF]).wait()
+    size_of = kv.at[:, :, pl.ds(0, (seq - seq_dev) * 2)]
+    whole = pltpu.make_async_remote_copy(size_of, size_of, bulk_sem.at[0], bulk_sem.at[1],
+                                         device_id={"tp": sibling}, device_id_type=MESH)
+    whole.wait_recv()
+    whole.wait_send()
+    store_new(0)
+    store_new(1)
 
 
 def flush_kernel(*refs):
@@ -412,14 +414,10 @@
                 *[pltpu.VMEM((2 * layers, chips, batch, 1, piece), jnp.float32)] * 3,
                 pltpu.VMEM((2 * layers, 2, chips, batch, 1, piece), jnp.float32),
                 pltpu.SemaphoreType.DMA((RING,)),
-                pltpu.SemaphoreType.DMA((layers,)),
-                pltpu.SemaphoreType.DMA((4,)),
-                pltpu.SemaphoreType.DMA((4,)),
-                pltpu.SemaphoreType.DMA((4,)),
-                pltpu.SemaphoreType.DMA((4,)),
-                pltpu.SemaphoreType.DMA((4,)),
-                pltpu.SemaphoreType.DMA((STEPS,)),
-                pltpu.SemaphoreType.DMA((STEPS,)),
+                pltpu.SemaphoreType.DMA((7,)),
+                pltpu.SemaphoreType.DMA((2,)),
+                pltpu.SemaphoreType.DMA((2,)),
+                pltpu.SemaphoreType.DMA((5,)),
             ],
             compiler_params=pltpu.CompilerParams(
                 collective_id=0, has_side_effects=True, vmem_limit_bytes=44 * 1024 * 1024),

time: 151 us -> 150 us (level)
  no operation moved by 1% of the time
where the time goes in v4:
time: 150 us
  Pallas kernels  150 us (100%)
    pallas_call x1, Pallas kernels, per_device(): pl.pallas_call(functools.partial(kernel, cfg), in_specs=[any_spec] * 19,...  145 us
    pallas_call x1, Pallas kernels, per_device(): pl.pallas_call(flush_kernel, in_specs=[vmem_spec] * 5, out_specs=[any_spe...  4.98 us

profile of v4, /device:TPU:113, one launch (start us, length us, event | category | flops | bytes accessed | tf_op | source)
XLA Modules:
  0.0 150.3 jit_solution(14344624353592919757)
XLA Ops:
  0.6 144.6 %shard_map.182 = (bf16[3,1024,2,2,128]{4,3,2,1,0:T(2,128)(2,1)S(1)}, bf16[3,1024,2,2,128]{4,3,2,1,0:T(2,128)(2,1)S(1)}, bf16[3,1152,2,2,128]{4,3,2,1,0:T(2,128)(...) custom-call(bf16[3,128,2,2,4,2,128]{6,5,4,3,2,1,0:T(2,128)(2,1)} %bitcast.28, ...), custom_call_target="tpu_custom_call" | custom-call | tf_op jit(solution)/shard_map/pallas_call | solution.py:392
  145.3 5.0 %shard_map.183 = (bf16[3,1024,2,2,128]{4,3,2,1,0:T(2,128)(2,1)}, bf16[3,1024,2,2,128]{4,3,2,1,0:T(2,128)(2,1)}, bf16[3,1152,2,2,128]{4,3,2,1,0:T(2,128)(2,1)}, b...) custom-call(bf16[3,1024,2,2,128]{4,3,2,1,0:T(2,128)(2,1)S(1)} %get-tuple-element.15.refs_0_, ...), custom_call_target="tpu_custom_call" | custom-call | tf_op jit(solution)/shard_map/pallas_call | solution.py:426

commit v5 on v4

--- a/solution.py
+++ b/solution.py
@@ -21,7 +21,7 @@
 CHUNK = 512
 SPLITS = 4
 FIRST_UNITS = 6
-ROUND_UNITS = (2, 2, 2, 2, 6, 2, 2, 2, 2, 2, 2, 6, 2, 2)
+ROUND_UNITS = (2, 3, 2, 2, 6, 2, 2, 2, 3, 2, 2, 6, 2, 2)
 ROUNDS = 7
 
 
@@ -92,7 +92,7 @@
     span = seq_dev // SPLITS
     units = [(c, b, f) for c in range(4) for b in range(batch) for f in range(SPLITS)]
     chips = groups // 2
-    order = [(dx, dc) for dc in range(2) for dx in (1, chips - 1, *range(2, chips - 1))] + [(0, 1)]
+    order = [(0, 1)] + [(dx, dc) for dc in range(2) for dx in (1, chips - 1, *range(2, chips - 1))]
     chip, core = me // 2, me % 2
 
     def peer(dx, dc):
@@ -135,7 +135,7 @@
             load(view_of(c, me, b, 0, seq_dev), cache_out[c].at[b, pl.ds(me * seq_dev, seq_dev)], SELF)
 
     sibling = chip * 2 + 1 - core
-    turns = {"pair": 0, "cross": 0, "all": 0}
+    turns = {"pair": 0, "cross": 0}
     pending = []
 
     def start_round(kind, copies, size_of):
@@ -144,7 +144,7 @@
         turn = turns[kind]
         turns[kind] += 1
         s_sem = r_send.at[sum(turns.values()) % 2]
-        r_sem = r_recv.at[{"pair": 0, "cross": 2, "all": 4}[kind] + (turn % 2 if kind != "all" else 0)]
+        r_sem = r_recv.at[{"pair": 0, "cross": 2}[kind] + turn % 2]
         for src, dst, device in copies:
             pltpu.make_async_remote_copy(src, dst, s_sem, r_sem, device_id={"tp": device}, device_id_type=MESH).start()
         pending.append(pltpu.make_async_remote_copy(size_of, size_of, s_sem, r_sem,
@@ -271,14 +271,13 @@
         l_loc = fold(ex, jnp.add)
         l_loc = jnp.where(own, l_loc + jnp.exp(s_new - m_loc), l_loc)
         mine = lane // heads == row
-        st_all[layer, me] = jnp.concatenate(
+        st_all[layer, core, chip] = jnp.concatenate(
             [jnp.sum(jnp.where(mine, t, 0.0), axis=0, keepdims=True) for t in (m_loc, l_loc)], axis=0)
-        got = start_round("all", [(st_all.at[layer, me], st_all.at[layer, me], (me + k) % groups) for k in range(1, groups)],
-                          st_all.at[layer, pl.ds(0, groups - 1)])
-        bulk(ROUND_UNITS[rnd + 1])
-        got.wait_recv()
+        gather_cross(st_all.at[layer], ROUND_UNITS[rnd + 1])
+        gather_pair(st_all.at[layer])
+
         def unpack(s, n):
-            return fold(jnp.where(mine, jnp.broadcast_to(st_all[layer, s, n:n + 1, :], (ROWS, LANES)), 0.0), jnp.add)
+            return fold(jnp.where(mine, jnp.broadcast_to(st_all[layer, s % 2, s // 2, n:n + 1, :], (ROWS, LANES)), 0.0), jnp.add)
 
         ms = [unpack(s, 0) for s in range(groups)]
         ls = [unpack(s, 1) for s in range(groups)]
@@ -355,9 +354,11 @@
 
 def flush_kernel(*refs):
     n = (len(refs) - 1) // 2
-    copies = [pltpu.make_async_copy(refs[i], refs[n + i], refs[-1].at[i]) for i in range(n)]
-    for c in copies:
-        c.start()
+    pairs = [(refs[i].at[b], refs[n + i].at[b]) for i in range(n - 1) for b in range(refs[i].shape[0])]
+    pairs.append((refs[n - 1], refs[2 * n - 1]))
+    copies = [pltpu.make_async_copy(src, dst, refs[-1].at[i]) for i, (src, dst) in enumerate(pairs)]
+    for i, c in enumerate(copies):
+        c.start(priority=i % 2)
     for c in copies:
         c.wait()
 
@@ -407,7 +408,7 @@
                 pltpu.VMEM((ROWS, width), jnp.bfloat16),
                 pltpu.VMEM((2 * ff_dev // CHUNK, ROWS, CHUNK), jnp.float32),
                 pltpu.VMEM((layers, 2, chips, batch, 2, head_dim), jnp.bfloat16),
-                pltpu.VMEM((layers, groups, 2, LANES), jnp.float32),
+                pltpu.VMEM((layers, 2, chips, 2, LANES), jnp.float32),
                 pltpu.VMEM((layers, 2, chips, batch, 2, head_dim), jnp.float32),
                 *[pltpu.VMEM((layers, chips, batch, 2, head_dim), jnp.float32)] * 3,
                 pltpu.VMEM((2 * layers, 2, chips, batch, 1, piece), jnp.float32),
@@ -417,7 +418,7 @@
                 pltpu.SemaphoreType.DMA((7,)),
                 pltpu.SemaphoreType.DMA((2,)),
                 pltpu.SemaphoreType.DMA((2,)),
-                pltpu.SemaphoreType.DMA((5,)),
+                pltpu.SemaphoreType.DMA((4,)),
             ],
             compiler_params=pltpu.CompilerParams(
                 collective_id=0, has_side_effects=True, vmem_limit_bytes=44 * 1024 * 1024),
@@ -428,7 +429,7 @@
             in_specs=[vmem_spec] * 5,
             out_specs=[any_spec] * 5,
             out_shape=[jax.ShapeDtypeStruct(y.shape, y.dtype) for y in res],
-            scratch_shapes=[pltpu.SemaphoreType.DMA((5,))],
+            scratch_shapes=[pltpu.SemaphoreType.DMA((4 * batch + 1,))],
             compiler_params=pltpu.CompilerParams(has_side_effects=True, vmem_limit_bytes=1024 * 1024),
         )(*held)
         outs = [y.transpose(0, 1, 3, 2, 4).reshape(batch, y.shape[1], 2, head_dim) for y in res[:4]]

time: 150 us -> 150 us (level)
  no operation moved by 1% of the time
where the time goes in v5:
time: 150 us
  Pallas kernels  149 us (99%)
    pallas_call x1, Pallas kernels, per_device(): pl.pallas_call(functools.partial(kernel, cfg), in_specs=[any_spec] * 19,...  145 us
    pallas_call x1, Pallas kernels, per_device(): pl.pallas_call(flush_kernel, in_specs=[vmem_spec] * 5, out_specs=[any_spe...  4.93 us

profile of v5, /device:TPU:113, one launch (start us, length us, event | category | flops | bytes accessed | tf_op | source)
XLA Modules:
  0.0 150.1 jit_solution(6256620547096823590)
XLA Ops:
  0.6 144.5 %shard_map.182 = (bf16[3,1024,2,2,128]{4,3,2,1,0:T(2,128)(2,1)S(1)}, bf16[3,1024,2,2,128]{4,3,2,1,0:T(2,128)(2,1)S(1)}, bf16[3,1152,2,2,128]{4,3,2,1,0:T(2,128)(...) custom-call(bf16[3,128,2,2,4,2,128]{6,5,4,3,2,1,0:T(2,128)(2,1)} %bitcast.28, ...), custom_call_target="tpu_custom_call" | custom-call | tf_op jit(solution)/shard_map/pallas_call | solution.py:393
  145.2 4.9 %shard_map.183 = (bf16[3,1024,2,2,128]{4,3,2,1,0:T(2,128)(2,1)}, bf16[3,1024,2,2,128]{4,3,2,1,0:T(2,128)(2,1)}, bf16[3,1152,2,2,128]{4,3,2,1,0:T(2,128)(2,1)}, b...) custom-call(bf16[3,1024,2,2,128]{4,3,2,1,0:T(2,128)(2,1)S(1)} %get-tuple-element.15.refs_0_, ...), custom_call_target="tpu_custom_call" | custom-call | tf_op jit(solution)/shard_map/pallas_call | solution.py:427

commit v6 on v5

--- a/solution.py
+++ b/solution.py
@@ -20,8 +20,8 @@
 RING = 8
 CHUNK = 512
 SPLITS = 4
-FIRST_UNITS = 6
-ROUND_UNITS = (2, 3, 2, 2, 6, 2, 2, 2, 3, 2, 2, 6, 2, 2)
+FIRST_UNITS = 5
+ROUND_UNITS = (2, 3, 2, 2, 6, 2, 3, 2, 3, 2, 2, 6, 2, 2)
 ROUNDS = 7
 
 

time: 150 us -> 150 us (level)
  no operation moved by 1% of the time
where the time goes in v6:
time: 150 us
  Pallas kernels  149 us (99%)
    pallas_call x1, Pallas kernels, per_device(): pl.pallas_call(functools.partial(kernel, cfg), in_specs=[any_spec] * 19,...  144 us
    pallas_call x1, Pallas kernels, per_device(): pl.pallas_call(flush_kernel, in_specs=[vmem_spec] * 5, out_specs=[any_spe...  4.93 us

profile of v6, /device:TPU:113, one launch (start us, length us, event | category | flops | bytes accessed | tf_op | source)
XLA Modules:
  0.0 150.0 jit_solution(11114658682515322813)
XLA Ops:
  0.6 144.4 %shard_map.182 = (bf16[3,1024,2,2,128]{4,3,2,1,0:T(2,128)(2,1)S(1)}, bf16[3,1024,2,2,128]{4,3,2,1,0:T(2,128)(2,1)S(1)}, bf16[3,1152,2,2,128]{4,3,2,1,0:T(2,128)(...) custom-call(bf16[3,128,2,2,4,2,128]{6,5,4,3,2,1,0:T(2,128)(2,1)} %bitcast.28, ...), custom_call_target="tpu_custom_call" | custom-call | tf_op jit(solution)/shard_map/pallas_call | solution.py:393
  145.0 4.9 %shard_map.183 = (bf16[3,1024,2,2,128]{4,3,2,1,0:T(2,128)(2,1)}, bf16[3,1024,2,2,128]{4,3,2,1,0:T(2,128)(2,1)}, bf16[3,1152,2,2,128]{4,3,2,1,0:T(2,128)(2,1)}, b...) custom-call(bf16[3,1024,2,2,128]{4,3,2,1,0:T(2,128)(2,1)S(1)} %get-tuple-element.15.refs_0_, ...), custom_call_target="tpu_custom_call" | custom-call | tf_op jit(solution)/shard_map/pallas_call | solution.py:427
